TPU v7x, 256 devices: a whole 4x4x8 slice. The times are simulated.
256 devices in a mesh: grp: 2 (over y_lo), mesh: 128 (over z, x, y_hi, core).
Axes of the slice: x: 4, y: 4 (y_hi: 2, y_lo: 2; y = y_hi * 2 + y_lo), z: 8, core: 2. Of those that a mesh axis runs over, the one named last changes fastest.
Arguments:
- state: float32 [2, 5, 2048, 4096], P('grp', None, 'mesh'), may hold values from -6 to 6
- burn_rate: float32 [2, 2048, 4096], P('grp', 'mesh'), may hold values from 0.1 to 1
- face_map: int32 [2, 128, 1024], P('grp', 'mesh'), may hold values from 0 to 1023, as said below
Outputs:
- new_state: float32 [2, 5, 2048, 4096], P('grp', None, 'mesh')
- head: float32 [2, 2048, 4096], P('grp', 'mesh')
Inputs may be any that keep to these rules, and one draw needn't show every extreme that they name: `face_map`: entry k * 64 + j of a mesh names the cell of its partner's interface plane that feeds its ghost cell (k, j).
All inputs are finite; a program needn't handle non-finite values.
Results may differ from a plain program's by a relative error of at most 0.00025.
Values sent between devices are 32-bit elements; how exact they have to be, the bound alone decides.
A program may use at most 64 MiB of HBM per device.

v0:
```python
import jax
import jax.numpy as jnp
from jax import lax
from jax.sharding import PartitionSpec as P

NX = 64
NY = 64
FIELDS = 5
SECTIONS = 2
ITERS = 3


COURANT = 0.1
DIFFUSION = 0.05
STOICHIOMETRY = 2.0
EXPANSION = 1.0


def with_halo(block, sides, width):
    for axis, dim in sides:
        count = lax.axis_size(axis)
        forward = [(i, i + 1) for i in range(count - 1)]
        backward = [(target, source) for source, target in forward]
        low = lax.ppermute(
            lax.slice_in_dim(block, block.shape[dim] - width, None, axis=dim), axis, forward
        )
        high = lax.ppermute(lax.slice_in_dim(block, 0, width, axis=dim), axis, backward)
        block = jnp.concatenate([low, block, high], axis=dim)
    return block


def from_partner(block, axis, bit):
    count = lax.axis_size(axis)
    route = []
    for low in range(count):
        high = low | 1 << bit
        if high != low and high < count:
            route += [(low, high), (high, low)]
    return lax.ppermute(block, axis, route)


def sine_table(length):
    places = jnp.arange(length, dtype=jnp.float32) + 1.0
    angles = jnp.pi * places[:, None] * places[None, :] / (length + 1)
    return jnp.sin(angles) * jnp.sqrt(2.0 / (length + 1))


def mode_values(length):
    places = jnp.arange(length, dtype=jnp.float32) + 1.0
    return 2.0 - 2.0 * jnp.cos(jnp.pi * places / (length + 1))


def poisson_solve(source):
    table_z = sine_table(source.shape[1])
    table_x = sine_table(source.shape[2])
    table_y = sine_table(source.shape[3])
    precise = lax.Precision.HIGHEST
    spectral = jnp.einsum("ck,mkij->mcij", table_z, source, precision=precise)
    spectral = jnp.einsum("ai,mcij->mcaj", table_x, spectral, precision=precise)
    spectral = jnp.einsum("mcaj,jb->mcab", spectral, table_y, precision=precise)
    modes = (
        mode_values(source.shape[1])[:, None, None]
        + mode_values(source.shape[2])[None, :, None]
        + mode_values(source.shape[3])[None, None, :]
    )
    spectral = spectral / modes[None]
    solved = jnp.einsum("ck,mcab->mkab", table_z, spectral, precision=precise)
    solved = jnp.einsum("ai,mkab->mkib", table_x, solved, precision=precise)
    return jnp.einsum("mkib,jb->mkij", solved, table_y, precision=precise)


def tendency(zpadded, x_low, x_high, burning):
    centre = zpadded[:, 2:-2]
    xpadded = jnp.concatenate([x_low[:, :, None, :], centre, x_high[:, :, None, :]], axis=2)
    ypadded = jnp.pad(centre, ((0, 0), (0, 0), (0, 0), (1, 1)))
    east, west = (xpadded[:, :, 2:], xpadded[:, :, :-2])
    north, south = (ypadded[..., 2:], ypadded[..., :-2])
    above, below = (zpadded[:, 3:-1], zpadded[:, 1:-3])
    above_two, below_two = (zpadded[:, 4:], zpadded[:, :-4])
    grad_x = 0.5 * (east - west)
    grad_y = 0.5 * (north - south)
    grad_z = (8.0 * (above - below) - (above_two - below_two)) / 12.0
    laplace = east + west + north + south + above + below - 6.0 * centre
    advection = centre[0] * grad_x + centre[1] * grad_y + centre[2] * grad_z
    reaction = burning * centre[3] * centre[4]
    change = -COURANT * advection + DIFFUSION * laplace
    change = change.at[3].add(-reaction).at[4].add(-STOICHIOMETRY * reaction)
    divergence = grad_x[0] + grad_y[1] + 0.5 * (above[2] - below[2])
    return (change, EXPANSION * reaction - divergence)


def with_ghosts(source, z_low, z_high, x_low, x_high):
    source = source.at[:, 0].add(z_low).at[:, -1].add(z_high)
    return source.at[:, :, 0, :].add(x_low).at[:, :, -1, :].add(x_high)


def correct(fields, pressure, z_low, z_high, x_low, x_high):
    xpadded = jnp.concatenate([x_low[:, None, :], pressure, x_high[:, None, :]], axis=1)
    ypadded = jnp.pad(pressure, ((0, 0), (0, 0), (1, 1)))
    zpadded = jnp.concatenate([z_low[None], pressure, z_high[None]], axis=0)
    grad_x = 0.5 * (xpadded[:, 2:] - xpadded[:, :-2])
    grad_y = 0.5 * (ypadded[..., 2:] - ypadded[..., :-2])
    grad_z = 0.5 * (zpadded[2:] - zpadded[:-2])
    return jnp.concatenate(
        [
            fields[0:1] - grad_x[None],
            fields[1:2] - grad_y[None],
            fields[2:3] - grad_z[None],
            fields[3:],
        ],
        axis=0,
    )


def own_plane(arrays, is_fine):
    plane = jnp.where(is_fine, arrays[..., -1, :], arrays[..., 0, :])
    return plane.reshape(plane.shape[:-2] + (plane.shape[-2] * plane.shape[-1],))


def place_ghost(received, mapping, is_fine):
    picked = jnp.take(received, mapping, axis=-1)
    picked = picked.reshape(received.shape[:-1] + (received.shape[-1] // NY, NY))
    zeros = jnp.zeros_like(picked)
    return (jnp.where(is_fine, zeros, picked), jnp.where(is_fine, picked, zeros))


def shards(state, burn_rate, face_map):
    is_fine = lax.axis_index("grp") == 0
    height = state.shape[2]
    initial = state[0].reshape(FIELDS, height, NX, NY)
    burning = burn_rate[0].reshape(height, NX, NY)
    mapping = face_map[0, 0]

    def head_ghosts(pressure):
        padded = with_halo(pressure[0].reshape(height, NX * NY), (("mesh", 0),), 1)
        received = from_partner(own_plane(pressure, is_fine), "grp", 0)
        x_low, x_high = place_ghost(received, mapping, is_fine)
        return (padded[0].reshape(1, NX, NY), padded[-1].reshape(1, NX, NY), x_low, x_high)

    current = initial
    pressure = jnp.zeros((1, height, NX, NY), state.dtype)
    for section_no in range(SECTIONS):
        padded = with_halo(current.reshape(FIELDS, height, NX * NY), (("mesh", 1),), 2).reshape(
            FIELDS, height + 4, NX, NY
        )
        received = from_partner(own_plane(current, is_fine), "grp", 0)
        x_low, x_high = place_ghost(received, mapping, is_fine)
        change, source = tendency(padded, x_low, x_high, burning)
        if section_no == 0:
            predicted = current + change
        else:
            predicted = 0.5 * (initial + current + change)
        source = source[None]
        zero_pressure = jnp.zeros((1, height, NX, NY), state.dtype)
        zero_layer = jnp.zeros((1, NX, NY), state.dtype)
        zero_side = jnp.zeros((1, height, NY), state.dtype)

        def sweep_once(sweep, carry):
            ghosts = carry[1]
            solved = poisson_solve(with_ghosts(source, ghosts[0], ghosts[1], ghosts[2], ghosts[3]))
            return (solved, head_ghosts(solved))

        pressure, ghosts = lax.fori_loop(
            0, ITERS, sweep_once, (zero_pressure, (zero_layer, zero_layer, zero_side, zero_side))
        )
        current = correct(
            predicted, pressure[0], ghosts[0][0], ghosts[1][0], ghosts[2][0], ghosts[3][0]
        )
    return (current.reshape(1, FIELDS, height, NX * NY), pressure.reshape(1, height, NX * NY))


def solution(mesh):
    placed = (P("grp", None, "mesh", None), P("grp", "mesh", None), P("grp", "mesh", None))
    return jax.shard_map(
        shards,
        mesh=mesh,
        in_specs=placed,
        out_specs=(P("grp", None, "mesh", None), P("grp", "mesh", None)),
        check_vma=False,
    )
```

profile of v0, /device:TPU:128, one launch (start us, length us, event | category | flops | bytes accessed | tf_op | source)
XLA Modules:
  0.0 303.0 jit_solution(1360061391204217888)
XLA Ops:
  0.6 2.1 fusion.159
  4.7 9.4 %collective-permute-start.7 = (f32[5,2,4096]{2,1,0:T(2,128)}, f32[5,2,4096]{2,1,0:T(2,128)}, u32[]{:S(2)}, u32[]{:S(2)}) collective-permute-start(f32[5,2,4096]{2,1,0:T(2,128)} %get-tuple-element.617), channel_id=1, source_target_pairs={{1,0},{2,1},{3,2},{4,3},{5,4},{6,5},{7,6},{8,7},{9,8},{10,9},{11,1... | collective-permute-start | bytes 491528 | tf_op jit(solution)/shard_map/ppermute | solution.py:27
  14.1 2.2 reshape_squeeze.6
  19.0 2.2 fusion.158
  21.2 2.0 mul.567
  23.1 2.0 mul.561
  29.4 5.1 %gather_fusion.2 = f32[1024,5]{1,0:T(8,128)} fusion(f32[5,1024]{0,1:T(8,128)} %collective-permute-done.6, s32[1024]{0:T(1024)S(1)} %fusion.152), kind=kCustom, calls=%fused_computation.clone | custom fusion | bytes 45056 | tf_op jit(solution)/shard_map/jit(_take)/gather | solution.py:121
  34.4 2.3 bitcast_select_fusion.2
  41.7 3.0 %constant_dynamic-update-slice_fusion.1 = (f32[5,18,64,64]{3,2,1,0:T(8,128)}, f32[5,18,64,64]{3,2,1,0:T(8,128)}) fusion(f32[5,16,64,64]{3,2,1,0:T(8,128)S(1)} %reshape_squeeze.6, f32[5,18,64,64]{3,2,1,0:T(8,128)} %constant_dynamic-update-slice_fusion.3), kind=kLoop, calls=%fused_computation.258 | loop fusion | bytes 6553600
  46.7 6.7 %fusion.121 = (f32[5,16,64,64]{3,2,1,0:T(8,128)S(1)}, f32[5,16,64,64]{3,2,1,0:T(8,128)S(1)}, f32[5,16,64,64]{3,2,1,0:T(8,128)S(1)}) fusion(f32[5,18,64,64]{3,2,1,0:T(8,128)} %get-tuple-element.609, f32[5,18,64,64]{3,2,1,0:T(8,128)} %constant_dynamic-update-slice_fusion, f32[5,16,64,64]{3,2,1,0:T(8,128)S(1)} %reshape_squeeze.6, ...), kind=kLoop, calls=%fused_computation.181 | loop fusion | flops 7536640 | bytes 11313152 | tf_op jit(solution)/shard_map/add | solution.py:86
  60.6 89.5 %while.54 = (s32[]{:T(128)}, f32[1,16,64,64]{3,2,1,0:T(8,128)}, f32[1,64,64]{2,1,0:T(8,128)S(1)}, f32[1,64,64]{2,1,0:T(8,128)S(1)}, f32[1,16,64]{2,1,0:T(8,128)S...) while((s32[]{:T(128)}, f32[1,16,64,64]{3,2,1,0:T(8,128)}, ...), condition=%wide.region_1.4_spmd, body=%wide.region_0.0_spmd.sunk | while | flops 226700256 | bytes 5959731 | solution.py:163
  68.7 1.9 collective-permute-start
  70.7 9.4 %collective-permute-start.1 = (f32[1,4096]{1,0:T(1,128)S(1)}, f32[1,4096]{1,0:T(1,128)S(1)}, u32[]{:S(2)}, u32[]{:S(2)}) collective-permute-start(f32[1,4096]{1,0:T(1,128)S(1)} %slice.945), channel_id=1, source_target_pairs={{1,0},{2,1},{3,2},{4,3},{5,4},{6,5},{7,6},{8,7},{9,8},{10,9},{11,1... | collective-permute-start | bytes 49160 | tf_op jit(solution)/shard_map/while/body/eval_jaxpr/ppermute | solution.py:27
  80.7 3.2 %collective-permute-done.2 = f32[1,1024]{1,0:T(1,128)S(1)} collective-permute-done((f32[1,1024]{1,0:T(1,128)S(1)}, f32[1,1024]{1,0:T(1,128)S(1)}, u32[]{:S(2)}, u32[]{:S(2)}) %collective-permute-start.2) | collective-permute-done | bytes 4128 | tf_op jit(solution)/shard_map/while/body/eval_jaxpr/ppermute | solution.py:39
  83.8 4.5 %gather_fusion = f32[1024]{0:T(1024)S(1)} fusion(f32[1024]{0:T(1024)S(1)} %bitcast.273, s32[1024]{0:T(1024)S(1)} %fusion.221), kind=kCustom, calls=%fused_computation.1.clone.clone.1 | custom fusion | bytes 12288 | tf_op jit(solution)/shard_map/while/body/eval_jaxpr/jit(_take)/gather | solution.py:121
  98.4 1.9 collective-permute-start
  100.5 9.4 %collective-permute-start.1 = (f32[1,4096]{1,0:T(1,128)S(1)}, f32[1,4096]{1,0:T(1,128)S(1)}, u32[]{:S(2)}, u32[]{:S(2)}) collective-permute-start(f32[1,4096]{1,0:T(1,128)S(1)} %slice.945), channel_id=1, source_target_pairs={{1,0},{2,1},{3,2},{4,3},{5,4},{6,5},{7,6},{8,7},{9,8},{10,9},{11,1... | collective-permute-start | bytes 49160 | tf_op jit(solution)/shard_map/while/body/eval_jaxpr/ppermute | solution.py:27
  110.4 3.2 %collective-permute-done.2 = f32[1,1024]{1,0:T(1,128)S(1)} collective-permute-done((f32[1,1024]{1,0:T(1,128)S(1)}, f32[1,1024]{1,0:T(1,128)S(1)}, u32[]{:S(2)}, u32[]{:S(2)}) %collective-permute-start.2) | collective-permute-done | bytes 4128 | tf_op jit(solution)/shard_map/while/body/eval_jaxpr/ppermute | solution.py:39
  113.6 4.5 %gather_fusion = f32[1024]{0:T(1024)S(1)} fusion(f32[1024]{0:T(1024)S(1)} %bitcast.273, s32[1024]{0:T(1024)S(1)} %fusion.221), kind=kCustom, calls=%fused_computation.1.clone.clone.1 | custom fusion | bytes 12288 | tf_op jit(solution)/shard_map/while/body/eval_jaxpr/jit(_take)/gather | solution.py:121
  128.2 1.9 collective-permute-start
  130.2 9.4 %collective-permute-start.1 = (f32[1,4096]{1,0:T(1,128)S(1)}, f32[1,4096]{1,0:T(1,128)S(1)}, u32[]{:S(2)}, u32[]{:S(2)}) collective-permute-start(f32[1,4096]{1,0:T(1,128)S(1)} %slice.945), channel_id=1, source_target_pairs={{1,0},{2,1},{3,2},{4,3},{5,4},{6,5},{7,6},{8,7},{9,8},{10,9},{11,1... | collective-permute-start | bytes 49160 | tf_op jit(solution)/shard_map/while/body/eval_jaxpr/ppermute | solution.py:27
  140.2 3.2 %collective-permute-done.2 = f32[1,1024]{1,0:T(1,128)S(1)} collective-permute-done((f32[1,1024]{1,0:T(1,128)S(1)}, f32[1,1024]{1,0:T(1,128)S(1)}, u32[]{:S(2)}, u32[]{:S(2)}) %collective-permute-start.2) | collective-permute-done | bytes 4128 | tf_op jit(solution)/shard_map/while/body/eval_jaxpr/ppermute | solution.py:39
  143.4 4.5 %gather_fusion = f32[1024]{0:T(1024)S(1)} fusion(f32[1024]{0:T(1024)S(1)} %bitcast.273, s32[1024]{0:T(1024)S(1)} %fusion.221), kind=kCustom, calls=%fused_computation.1.clone.clone.1 | custom fusion | bytes 12288 | tf_op jit(solution)/shard_map/while/body/eval_jaxpr/jit(_take)/gather | solution.py:121
  150.1 4.4 %multiply_bitcast_fusion.2 = (f32[16,64,64]{2,1,0:T(8,128)}, f32[1,16,64,64]{3,2,1,0:T(8,128)S(1)}, f32[16,64,64]{2,1,0:T(8,128)}, f32[1,16,64,64]{3,2,1,0:T(8,1...) fusion(f32[16,64,64]{2,1,0:T(8,128)} %bitcast.283, f32[16,1,64]{2,1,0:T(1,128)S(1)} %bitcast.302, ...), kind=kLoop, calls=%fused_computation.249 | loop fusion | flops 1048576 | bytes 2662400 | tf_op jit(solution)/shard_map/mul | solution.py:84
  157.3 3.1 %reshape.1127 = f32[5,16,4096]{2,1,0:T(8,128)} reshape(f32[5,16,64,64]{3,2,1,0:T(8,128)} %pad_maximum_fusion.11) | data formatting | bytes 2621440 | tf_op jit(solution)/shard_map/reshape | solution.py:143
  163.0 2.1 fusion.157
  167.0 2.4 collective-permute-start.11
  169.4 2.6 collective-permute-done.9
  172.1 5.1 %gather_fusion.3 = f32[1024,5]{1,0:T(8,128)} fusion(f32[5,1024]{0,1:T(8,128)} %collective-permute-done.9, s32[1024]{0:T(1024)S(1)} %fusion.152), kind=kCustom, calls=%fused_computation.2.clone | custom fusion | bytes 45056 | tf_op jit(solution)/shard_map/jit(_take)/gather | solution.py:121
  177.1 2.2 bitcast_select_fusion
  181.9 4.3 %fusion.123 = f32[5,16,64,64]{3,2,1,0:T(8,128)} fusion(f32[5,16,1,64]{3,2,1,0:T(1,128)S(1)} %copy.39, f32[2,16,64,64]{3,2,1,0:T(8,128)} %slice.754, f32[1,16,64,64]{3,2,1,0:T(8,128)} %copy-done.4, f32[1,16,64,64]{3,2,1,0:T(8,128)} %copy-done.2, f32[1,16,64,64]{3,2,1,0:T(8,128)S(1)} %get-tuple-element.577, f32[5,16,1,64]{3,2,1,0:T(1,128)S(1)} %copy.40), kind=kLoop, calls=%fused_computation.192 | loop fusion | flops 2949120 | bytes 2662400 | tf_op jit(solution)/shard_map/sub | solution.py:80
  189.3 2.8 pad_maximum_fusion
  193.2 6.1 %fusion.116 = (f32[5,16,64,64]{3,2,1,0:T(8,128)}, f32[5,16,64,64]{3,2,1,0:T(8,128)}) fusion(f32[5,18,64,64]{3,2,1,0:T(8,128)S(1)} %get-tuple-element.607, f32[5,18,64,64]{3,2,1,0:T(8,128)S(1)} %get-tuple-element.606, f32[5,16,64,64]{3,2,1,0:T(8,128)S(1)} %copy-done.6, f32[16,64,64]{2,1,0:T(8,128)} %get-tuple-element.603, f32[16,64,64]{2,1,0:T(8,128)S(1)} %copy-done.19, ...), kind=kLoop, calls=%fused_computation.167 | loop fusion | flops 9502720 | bytes 11313152 | tf_op jit(solution)/shard_map/add | solution.py:86
  199.3 2.0 fusion.134
  206.5 86.3 %while.55 = (s32[]{:T(128)}, f32[1,16,64,64]{3,2,1,0:T(8,128)}, f32[1,64,64]{2,1,0:T(8,128)S(1)}, f32[1,64,64]{2,1,0:T(8,128)S(1)}, f32[1,16,64]{2,1,0:T(8,128)S...) while((s32[]{:T(128)}, f32[1,16,64,64]{3,2,1,0:T(8,128)}, ...), condition=%wide.region_3.6_spmd, body=%wide.region_2.5_spmd.sunk | while | flops 226700256 | bytes 5959731 | solution.py:163
  213.3 1.9 collective-permute-start.3
  215.4 9.4 %collective-permute-start.4 = (f32[1,4096]{1,0:T(1,128)S(1)}, f32[1,4096]{1,0:T(1,128)S(1)}, u32[]{:S(2)}, u32[]{:S(2)}) collective-permute-start(f32[1,4096]{1,0:T(1,128)S(1)} %slice.955), channel_id=1, source_target_pairs={{1,0},{2,1},{3,2},{4,3},{5,4},{6,5},{7,6},{8,7},{9,8},{10,9},{11,1... | collective-permute-start | bytes 49160 | tf_op jit(solution)/shard_map/while/body/eval_jaxpr/ppermute | solution.py:27
  225.3 3.2 %collective-permute-done.5 = f32[1,1024]{1,0:T(1,128)S(1)} collective-permute-done((f32[1,1024]{1,0:T(1,128)S(1)}, f32[1,1024]{1,0:T(1,128)S(1)}, u32[]{:S(2)}, u32[]{:S(2)}) %collective-permute-start.5) | collective-permute-done | bytes 4128 | tf_op jit(solution)/shard_map/while/body/eval_jaxpr/ppermute | solution.py:39
  228.5 4.5 %gather_fusion.1 = f32[1024]{0:T(1024)S(1)} fusion(f32[1024]{0:T(1024)S(1)} %bitcast.274, s32[1024]{0:T(1024)S(1)} %fusion.240), kind=kCustom, calls=%fused_computation.3.clone.clone.1 | custom fusion | bytes 12288 | tf_op jit(solution)/shard_map/while/body/eval_jaxpr/jit(_take)/gather | solution.py:121
  244.1 9.4 %collective-permute-start.4 = (f32[1,4096]{1,0:T(1,128)S(1)}, f32[1,4096]{1,0:T(1,128)S(1)}, u32[]{:S(2)}, u32[]{:S(2)}) collective-permute-start(f32[1,4096]{1,0:T(1,128)S(1)} %slice.955), channel_id=1, source_target_pairs={{1,0},{2,1},{3,2},{4,3},{5,4},{6,5},{7,6},{8,7},{9,8},{10,9},{11,1... | collective-permute-start | bytes 49160 | tf_op jit(solution)/shard_map/while/body/eval_jaxpr/ppermute | solution.py:27
  254.1 3.2 %collective-permute-done.5 = f32[1,1024]{1,0:T(1,128)S(1)} collective-permute-done((f32[1,1024]{1,0:T(1,128)S(1)}, f32[1,1024]{1,0:T(1,128)S(1)}, u32[]{:S(2)}, u32[]{:S(2)}) %collective-permute-start.5) | collective-permute-done | bytes 4128 | tf_op jit(solution)/shard_map/while/body/eval_jaxpr/ppermute | solution.py:39
  257.3 4.5 %gather_fusion.1 = f32[1024]{0:T(1024)S(1)} fusion(f32[1024]{0:T(1024)S(1)} %bitcast.274, s32[1024]{0:T(1024)S(1)} %fusion.240), kind=kCustom, calls=%fused_computation.3.clone.clone.1 | custom fusion | bytes 12288 | tf_op jit(solution)/shard_map/while/body/eval_jaxpr/jit(_take)/gather | solution.py:121
  272.9 9.4 %collective-permute-start.4 = (f32[1,4096]{1,0:T(1,128)S(1)}, f32[1,4096]{1,0:T(1,128)S(1)}, u32[]{:S(2)}, u32[]{:S(2)}) collective-permute-start(f32[1,4096]{1,0:T(1,128)S(1)} %slice.955), channel_id=1, source_target_pairs={{1,0},{2,1},{3,2},{4,3},{5,4},{6,5},{7,6},{8,7},{9,8},{10,9},{11,1... | collective-permute-start | bytes 49160 | tf_op jit(solution)/shard_map/while/body/eval_jaxpr/ppermute | solution.py:27
  282.9 3.2 %collective-permute-done.5 = f32[1,1024]{1,0:T(1,128)S(1)} collective-permute-done((f32[1,1024]{1,0:T(1,128)S(1)}, f32[1,1024]{1,0:T(1,128)S(1)}, u32[]{:S(2)}, u32[]{:S(2)}) %collective-permute-start.5) | collective-permute-done | bytes 4128 | tf_op jit(solution)/shard_map/while/body/eval_jaxpr/ppermute | solution.py:39
  286.0 4.5 %gather_fusion.1 = f32[1024]{0:T(1024)S(1)} fusion(f32[1024]{0:T(1024)S(1)} %bitcast.274, s32[1024]{0:T(1024)S(1)} %fusion.240), kind=kCustom, calls=%fused_computation.3.clone.clone.1 | custom fusion | bytes 12288 | tf_op jit(solution)/shard_map/while/body/eval_jaxpr/jit(_take)/gather | solution.py:121
  292.8 2.0 reshape.1129
  294.8 3.3 %fusion.131 = (f32[1,16,64,64]{3,2,1,0:T(8,128)S(1)}, f32[1,16,64,64]{3,2,1,0:T(8,128)S(1)}, f32[1,16,64,64]{3,2,1,0:T(8,128)S(1)}) fusion(f32[16,64,64]{2,1,0:T(8,128)} %bitcast.279, f32[16,1,64]{2,1,0:T(1,128)S(1)} %bitcast.300, f32[16,1,64]{2,1,0:T(1,128)S(1)} %bitcast.301, f32[5,16,64,64]{3,2,1,0:T(8,128)} %copy-done.10, ...), kind=kLoop, calls=%fused_computation.204 | loop fusion | flops 851968 | bytes 1875968 | tf_op jit(solution)/shard_map/sub | solution.py:106
  299.9 3.1 %reshape.1128 = f32[1,5,16,4096]{3,2,1,0:T(8,128)} reshape(f32[5,16,64,64]{3,2,1,0:T(8,128)} %pad_maximum_fusion.12) | data formatting | bytes 2621440 | tf_op jit(solution)/shard_map/reshape | solution.py:169
  (333 shorter events, 108.5 us)
Async XLA Ops:
  2.8 37.1 %collective-permute-start.8 = (f32[5,2,4096]{2,1,0:T(2,128)}, f32[5,2,4096]{2,1,0:T(2,128)}, u32[]{:S(2)}, u32[]{:S(2)}) collective-permute-start(f32[5,2,4096]{2,1,0:T(2,128)} %get-tuple-element.618), channel_id=1, source_target_pairs={{0,1},{1,2},{2,3},{3,4},{4,5},{5,6},{6,7},{7,8},{8,9},{9,10},{10,1... | collective-permute-start | bytes 491528 | tf_op jit(solution)/shard_map/ppermute | solution.py:24
  4.7 40.1 %collective-permute-start.7 = (f32[5,2,4096]{2,1,0:T(2,128)}, f32[5,2,4096]{2,1,0:T(2,128)}, u32[]{:S(2)}, u32[]{:S(2)}) collective-permute-start(f32[5,2,4096]{2,1,0:T(2,128)} %get-tuple-element.617), channel_id=1, source_target_pairs={{1,0},{2,1},{3,2},{4,3},{5,4},{6,5},{7,6},{8,7},{9,8},{10,9},{11,1... | collective-permute-start | bytes 491528 | tf_op jit(solution)/shard_map/ppermute | solution.py:27
  16.3 4.8 %copy-start.20 = (s32[1,1,1024]{2,1,0:T(1,128)S(1)}, s32[1,1,1024]{2,1,0:T(1,128)}, u32[]{:S(2)}) copy-start(s32[1,1,1024]{2,1,0:T(1,128)} %param.37) | copy-start | bytes 12292
  17.4 12.0 %collective-permute-start.6 = (f32[5,1024]{0,1:T(8,128)}, f32[5,1024]{0,1:T(8,128)}, u32[]{:S(2)}, u32[]{:S(2)}) collective-permute-start(f32[5,1024]{0,1:T(8,128)} %bitcast.49), channel_id=1, source_target_pairs={{0,128},{128,0},{1,129},{129,1},{2,130},{130,2},{3,131},{131,3},{4... | collective-permute-start | bytes 61448 | tf_op jit(solution)/shard_map/ppermute | solution.py:39
  28.3 25.1 %copy-start.12 = (f32[1,16,64,64]{3,2,1,0:T(8,128)}, f32[1,16,64,64]{3,2,1,0:T(8,128)S(1)}, u32[]{:S(2)}) copy-start(f32[1,16,64,64]{3,2,1,0:T(8,128)S(1)} %reshape_squeeze.7) | copy-start | bytes 786436
  46.7 6.7 %copy-start.16 = (f32[1,16,64,64]{3,2,1,0:T(8,128)S(1)}, f32[1,16,64,64]{3,2,1,0:T(8,128)}, u32[]{:S(2)}) copy-start(f32[1,16,64,64]{3,2,1,0:T(8,128)} %squeeze.65) | copy-start | bytes 786436
  46.7 6.7 %copy-start.17 = (f32[1,16,64,64]{3,2,1,0:T(8,128)S(1)}, f32[1,16,64,64]{3,2,1,0:T(8,128)}, u32[]{:S(2)}) copy-start(f32[1,16,64,64]{3,2,1,0:T(8,128)} %squeeze.64) | copy-start | bytes 786436
  57.1 1.5 copy-start.9
  68.5 22.0 %copy-start.14 = (f32[16,64,64]{2,1,0:T(8,128)}, f32[16,64,64]{2,1,0:T(8,128)S(1)}, u32[]{:S(2)}) copy-start(f32[16,64,64]{2,1,0:T(8,128)S(1)} %fusion.218) | copy-start | bytes 786436 | tf_op jit(solution)/shard_map/while
  68.7 19.9 %collective-permute-start = (f32[1,4096]{1,0:T(1,128)S(1)}, f32[1,4096]{1,0:T(1,128)S(1)}, u32[]{:S(2)}, u32[]{:S(2)}) collective-permute-start(f32[1,4096]{1,0:T(1,128)S(1)} %slice.944), channel_id=1, source_target_pairs={{0,1},{1,2},{2,3},{3,4},{4,5},{5,6},{6,7},{7,8},{8,9},{9,10},{10,1... | collective-permute-start | bytes 49160 | tf_op jit(solution)/shard_map/while/body/eval_jaxpr/ppermute | solution.py:24
  70.7 19.1 %collective-permute-start.1 = (f32[1,4096]{1,0:T(1,128)S(1)}, f32[1,4096]{1,0:T(1,128)S(1)}, u32[]{:S(2)}, u32[]{:S(2)}) collective-permute-start(f32[1,4096]{1,0:T(1,128)S(1)} %slice.945), channel_id=1, source_target_pairs={{1,0},{2,1},{3,2},{4,3},{5,4},{6,5},{7,6},{8,7},{9,8},{10,9},{11,1... | collective-permute-start | bytes 49160 | tf_op jit(solution)/shard_map/while/body/eval_jaxpr/ppermute | solution.py:27
  80.2 3.6 %collective-permute-start.2 = (f32[1,1024]{1,0:T(1,128)S(1)}, f32[1,1024]{1,0:T(1,128)S(1)}, u32[]{:S(2)}, u32[]{:S(2)}) collective-permute-start(f32[1,1024]{1,0:T(1,128)S(1)} %select_n.349), channel_id=1, source_target_pairs={{0,128},{128,0},{1,129},{129,1},{2,130},{130,2},{3,131},{131,3},{4... | collective-permute-start | bytes 12296 | tf_op jit(solution)/shard_map/while/body/eval_jaxpr/ppermute | solution.py:39
  98.3 22.0 %copy-start.14 = (f32[16,64,64]{2,1,0:T(8,128)}, f32[16,64,64]{2,1,0:T(8,128)S(1)}, u32[]{:S(2)}) copy-start(f32[16,64,64]{2,1,0:T(8,128)S(1)} %fusion.218) | copy-start | bytes 786436 | tf_op jit(solution)/shard_map/while
  98.4 19.9 %collective-permute-start = (f32[1,4096]{1,0:T(1,128)S(1)}, f32[1,4096]{1,0:T(1,128)S(1)}, u32[]{:S(2)}, u32[]{:S(2)}) collective-permute-start(f32[1,4096]{1,0:T(1,128)S(1)} %slice.944), channel_id=1, source_target_pairs={{0,1},{1,2},{2,3},{3,4},{4,5},{5,6},{6,7},{7,8},{8,9},{9,10},{10,1... | collective-permute-start | bytes 49160 | tf_op jit(solution)/shard_map/while/body/eval_jaxpr/ppermute | solution.py:24
  100.5 19.1 %collective-permute-start.1 = (f32[1,4096]{1,0:T(1,128)S(1)}, f32[1,4096]{1,0:T(1,128)S(1)}, u32[]{:S(2)}, u32[]{:S(2)}) collective-permute-start(f32[1,4096]{1,0:T(1,128)S(1)} %slice.945), channel_id=1, source_target_pairs={{1,0},{2,1},{3,2},{4,3},{5,4},{6,5},{7,6},{8,7},{9,8},{10,9},{11,1... | collective-permute-start | bytes 49160 | tf_op jit(solution)/shard_map/while/body/eval_jaxpr/ppermute | solution.py:27
  109.9 3.6 %collective-permute-start.2 = (f32[1,1024]{1,0:T(1,128)S(1)}, f32[1,1024]{1,0:T(1,128)S(1)}, u32[]{:S(2)}, u32[]{:S(2)}) collective-permute-start(f32[1,1024]{1,0:T(1,128)S(1)} %select_n.349), channel_id=1, source_target_pairs={{0,128},{128,0},{1,129},{129,1},{2,130},{130,2},{3,131},{131,3},{4... | collective-permute-start | bytes 12296 | tf_op jit(solution)/shard_map/while/body/eval_jaxpr/ppermute | solution.py:39
  128.1 22.0 %copy-start.14 = (f32[16,64,64]{2,1,0:T(8,128)}, f32[16,64,64]{2,1,0:T(8,128)S(1)}, u32[]{:S(2)}) copy-start(f32[16,64,64]{2,1,0:T(8,128)S(1)} %fusion.218) | copy-start | bytes 786436 | tf_op jit(solution)/shard_map/while
  128.2 19.9 %collective-permute-start = (f32[1,4096]{1,0:T(1,128)S(1)}, f32[1,4096]{1,0:T(1,128)S(1)}, u32[]{:S(2)}, u32[]{:S(2)}) collective-permute-start(f32[1,4096]{1,0:T(1,128)S(1)} %slice.944), channel_id=1, source_target_pairs={{0,1},{1,2},{2,3},{3,4},{4,5},{5,6},{6,7},{7,8},{8,9},{9,10},{10,1... | collective-permute-start | bytes 49160 | tf_op jit(solution)/shard_map/while/body/eval_jaxpr/ppermute | solution.py:24
  130.2 19.1 %collective-permute-start.1 = (f32[1,4096]{1,0:T(1,128)S(1)}, f32[1,4096]{1,0:T(1,128)S(1)}, u32[]{:S(2)}, u32[]{:S(2)}) collective-permute-start(f32[1,4096]{1,0:T(1,128)S(1)} %slice.945), channel_id=1, source_target_pairs={{1,0},{2,1},{3,2},{4,3},{5,4},{6,5},{7,6},{8,7},{9,8},{10,9},{11,1... | collective-permute-start | bytes 49160 | tf_op jit(solution)/shard_map/while/body/eval_jaxpr/ppermute | solution.py:27
  139.7 3.6 %collective-permute-start.2 = (f32[1,1024]{1,0:T(1,128)S(1)}, f32[1,1024]{1,0:T(1,128)S(1)}, u32[]{:S(2)}, u32[]{:S(2)}) collective-permute-start(f32[1,1024]{1,0:T(1,128)S(1)} %select_n.349), channel_id=1, source_target_pairs={{0,128},{128,0},{1,129},{129,1},{2,130},{130,2},{3,131},{131,3},{4... | collective-permute-start | bytes 12296 | tf_op jit(solution)/shard_map/while/body/eval_jaxpr/ppermute | solution.py:39
  150.1 5.4 %copy-start = (f32[2,16,64,64]{3,2,1,0:T(8,128)S(1)}, f32[2,16,64,64]{3,2,1,0:T(8,128)}, u32[]{:S(2)}) copy-start(f32[2,16,64,64]{3,2,1,0:T(8,128)} %slice.754) | copy-start | bytes 1572868
  162.6 9.5 %collective-permute-start.9 = (f32[5,1024]{0,1:T(8,128)}, f32[5,1024]{0,1:T(8,128)}, u32[]{:S(2)}, u32[]{:S(2)}) collective-permute-start(f32[5,1024]{0,1:T(8,128)} %bitcast.297), channel_id=1, source_target_pairs={{0,128},{128,0},{1,129},{129,1},{2,130},{130,2},{3,131},{131,3},{4... | collective-permute-start | bytes 61448 | tf_op jit(solution)/shard_map/ppermute | solution.py:39
  165.1 21.1 %collective-permute-start.10 = (f32[5,2,4096]{2,1,0:T(2,128)S(1)}, f32[5,2,4096]{2,1,0:T(2,128)}, u32[]{:S(2)}, u32[]{:S(2)}) collective-permute-start(f32[5,2,4096]{2,1,0:T(2,128)S(1)} %get-tuple-element.610), channel_id=1, source_target_pairs={{1,0},{2,1},{3,2},{4,3},{5,4},{6,5},{7,6},{8,7},{9,8},{10,9},{11,1... | collective-permute-start | bytes 491528 | tf_op jit(solution)/shard_map/ppermute | solution.py:27
  167.0 20.3 %collective-permute-start.11 = (f32[5,2,4096]{2,1,0:T(2,128)}, f32[5,2,4096]{2,1,0:T(2,128)}, u32[]{:S(2)}, u32[]{:S(2)}) collective-permute-start(f32[5,2,4096]{2,1,0:T(2,128)} %get-tuple-element.611), channel_id=1, source_target_pairs={{0,1},{1,2},{2,3},{3,4},{4,5},{5,6},{6,7},{7,8},{8,9},{9,10},{10,1... | collective-permute-start | bytes 491528 | tf_op jit(solution)/shard_map/ppermute | solution.py:24
  181.9 4.3 %copy-start.21 = (f32[5,16,1,64]{3,2,1,0:T(1,128)}, f32[5,16,1,64]{3,2,1,0:T(1,128)S(1)}, u32[]{:S(2)}) copy-start(f32[5,16,1,64]{3,2,1,0:T(1,128)S(1)} %copy.40) | copy-start | bytes 61444
  189.2 2.8 copy-start.1
  189.2 2.8 copy-start.3
  189.2 2.9 copy-start.5
  189.2 3.7 %copy-start.6 = (f32[5,16,64,64]{3,2,1,0:T(8,128)S(1)}, f32[5,16,64,64]{3,2,1,0:T(8,128)}, u32[]{:S(2)}) copy-start(f32[5,16,64,64]{3,2,1,0:T(8,128)} %pad_maximum_fusion.11) | copy-start | bytes 3932164
  189.2 3.8 %copy-start.18 = (f32[16,64,64]{2,1,0:T(8,128)S(1)}, f32[16,64,64]{2,1,0:T(8,128)}, u32[]{:S(2)}) copy-start(f32[16,64,64]{2,1,0:T(8,128)} %get-tuple-element.576) | copy-start | bytes 786436
  189.2 4.0 %copy-start.19 = (f32[16,64,64]{2,1,0:T(8,128)S(1)}, f32[16,64,64]{2,1,0:T(8,128)}, u32[]{:S(2)}) copy-start(f32[16,64,64]{2,1,0:T(8,128)} %get-tuple-element.601) | copy-start | bytes 786436
  189.3 4.0 %copy-start.22 = (f32[5,16,1,64]{3,2,1,0:T(1,128)S(1)}, f32[5,16,1,64]{3,2,1,0:T(1,128)}, u32[]{:S(2)}) copy-start(f32[5,16,1,64]{3,2,1,0:T(1,128)} %copy-done.21) | copy-start | bytes 61444
  193.2 6.1 %copy-start.13 = (f32[1,16,64,64]{3,2,1,0:T(8,128)S(1)}, f32[1,16,64,64]{3,2,1,0:T(8,128)}, u32[]{:S(2)}) copy-start(f32[1,16,64,64]{3,2,1,0:T(8,128)} %copy-done.12) | copy-start | bytes 786436
  193.2 6.1 %copy-start.15 = (f32[5,2,64,64]{3,2,1,0:T(8,128)S(1)}, f32[5,2,64,64]{3,2,1,0:T(8,128)}, u32[]{:S(2)}) copy-start(f32[5,2,64,64]{3,2,1,0:T(8,128)} %concatenate.127) | copy-start | bytes 491524
  199.3 3.1 %copy-start.8 = (f32[5,16,64,64]{3,2,1,0:T(8,128)S(1)}, f32[5,16,64,64]{3,2,1,0:T(8,128)}, u32[]{:S(2)}) copy-start(f32[5,16,64,64]{3,2,1,0:T(8,128)} %get-tuple-element.574) | copy-start | bytes 3932164
  213.2 22.0 %copy-start.11 = (f32[16,64,64]{2,1,0:T(8,128)}, f32[16,64,64]{2,1,0:T(8,128)S(1)}, u32[]{:S(2)}) copy-start(f32[16,64,64]{2,1,0:T(8,128)S(1)} %fusion.237) | copy-start | bytes 786436 | tf_op jit(solution)/shard_map/while
  213.3 19.9 %collective-permute-start.3 = (f32[1,4096]{1,0:T(1,128)S(1)}, f32[1,4096]{1,0:T(1,128)S(1)}, u32[]{:S(2)}, u32[]{:S(2)}) collective-permute-start(f32[1,4096]{1,0:T(1,128)S(1)} %slice.954), channel_id=1, source_target_pairs={{0,1},{1,2},{2,3},{3,4},{4,5},{5,6},{6,7},{7,8},{8,9},{9,10},{10,1... | collective-permute-start | bytes 49160 | tf_op jit(solution)/shard_map/while/body/eval_jaxpr/ppermute | solution.py:24
  215.4 19.1 %collective-permute-start.4 = (f32[1,4096]{1,0:T(1,128)S(1)}, f32[1,4096]{1,0:T(1,128)S(1)}, u32[]{:S(2)}, u32[]{:S(2)}) collective-permute-start(f32[1,4096]{1,0:T(1,128)S(1)} %slice.955), channel_id=1, source_target_pairs={{1,0},{2,1},{3,2},{4,3},{5,4},{6,5},{7,6},{8,7},{9,8},{10,9},{11,1... | collective-permute-start | bytes 49160 | tf_op jit(solution)/shard_map/while/body/eval_jaxpr/ppermute | solution.py:27
  224.8 3.6 %collective-permute-start.5 = (f32[1,1024]{1,0:T(1,128)S(1)}, f32[1,1024]{1,0:T(1,128)S(1)}, u32[]{:S(2)}, u32[]{:S(2)}) collective-permute-start(f32[1,1024]{1,0:T(1,128)S(1)} %select_n.359), channel_id=1, source_target_pairs={{0,128},{128,0},{1,129},{129,1},{2,130},{130,2},{3,131},{131,3},{4... | collective-permute-start | bytes 12296 | tf_op jit(solution)/shard_map/while/body/eval_jaxpr/ppermute | solution.py:39
  242.0 22.0 %copy-start.11 = (f32[16,64,64]{2,1,0:T(8,128)}, f32[16,64,64]{2,1,0:T(8,128)S(1)}, u32[]{:S(2)}) copy-start(f32[16,64,64]{2,1,0:T(8,128)S(1)} %fusion.237) | copy-start | bytes 786436 | tf_op jit(solution)/shard_map/while
  242.1 19.9 %collective-permute-start.3 = (f32[1,4096]{1,0:T(1,128)S(1)}, f32[1,4096]{1,0:T(1,128)S(1)}, u32[]{:S(2)}, u32[]{:S(2)}) collective-permute-start(f32[1,4096]{1,0:T(1,128)S(1)} %slice.954), channel_id=1, source_target_pairs={{0,1},{1,2},{2,3},{3,4},{4,5},{5,6},{6,7},{7,8},{8,9},{9,10},{10,1... | collective-permute-start | bytes 49160 | tf_op jit(solution)/shard_map/while/body/eval_jaxpr/ppermute | solution.py:24
  244.1 19.1 %collective-permute-start.4 = (f32[1,4096]{1,0:T(1,128)S(1)}, f32[1,4096]{1,0:T(1,128)S(1)}, u32[]{:S(2)}, u32[]{:S(2)}) collective-permute-start(f32[1,4096]{1,0:T(1,128)S(1)} %slice.955), channel_id=1, source_target_pairs={{1,0},{2,1},{3,2},{4,3},{5,4},{6,5},{7,6},{8,7},{9,8},{10,9},{11,1... | collective-permute-start | bytes 49160 | tf_op jit(solution)/shard_map/while/body/eval_jaxpr/ppermute | solution.py:27
  253.6 3.6 %collective-permute-start.5 = (f32[1,1024]{1,0:T(1,128)S(1)}, f32[1,1024]{1,0:T(1,128)S(1)}, u32[]{:S(2)}, u32[]{:S(2)}) collective-permute-start(f32[1,1024]{1,0:T(1,128)S(1)} %select_n.359), channel_id=1, source_target_pairs={{0,128},{128,0},{1,129},{129,1},{2,130},{130,2},{3,131},{131,3},{4... | collective-permute-start | bytes 12296 | tf_op jit(solution)/shard_map/while/body/eval_jaxpr/ppermute | solution.py:39
  270.8 22.0 %copy-start.11 = (f32[16,64,64]{2,1,0:T(8,128)}, f32[16,64,64]{2,1,0:T(8,128)S(1)}, u32[]{:S(2)}) copy-start(f32[16,64,64]{2,1,0:T(8,128)S(1)} %fusion.237) | copy-start | bytes 786436 | tf_op jit(solution)/shard_map/while
  270.9 19.9 %collective-permute-start.3 = (f32[1,4096]{1,0:T(1,128)S(1)}, f32[1,4096]{1,0:T(1,128)S(1)}, u32[]{:S(2)}, u32[]{:S(2)}) collective-permute-start(f32[1,4096]{1,0:T(1,128)S(1)} %slice.954), channel_id=1, source_target_pairs={{0,1},{1,2},{2,3},{3,4},{4,5},{5,6},{6,7},{7,8},{8,9},{9,10},{10,1... | collective-permute-start | bytes 49160 | tf_op jit(solution)/shard_map/while/body/eval_jaxpr/ppermute | solution.py:24
  272.9 19.1 %collective-permute-start.4 = (f32[1,4096]{1,0:T(1,128)S(1)}, f32[1,4096]{1,0:T(1,128)S(1)}, u32[]{:S(2)}, u32[]{:S(2)}) collective-permute-start(f32[1,4096]{1,0:T(1,128)S(1)} %slice.955), channel_id=1, source_target_pairs={{1,0},{2,1},{3,2},{4,3},{5,4},{6,5},{7,6},{8,7},{9,8},{10,9},{11,1... | collective-permute-start | bytes 49160 | tf_op jit(solution)/shard_map/while/body/eval_jaxpr/ppermute | solution.py:27
  282.4 3.6 %collective-permute-start.5 = (f32[1,1024]{1,0:T(1,128)S(1)}, f32[1,1024]{1,0:T(1,128)S(1)}, u32[]{:S(2)}, u32[]{:S(2)}) collective-permute-start(f32[1,1024]{1,0:T(1,128)S(1)} %select_n.359), channel_id=1, source_target_pairs={{0,128},{128,0},{1,129},{129,1},{2,130},{130,2},{3,131},{131,3},{4... | collective-permute-start | bytes 12296 | tf_op jit(solution)/shard_map/while/body/eval_jaxpr/ppermute | solution.py:39
  292.8 5.3 %slice-start = ((f32[5,16,64,64]{3,2,1,0:T(8,128)}), f32[2,16,64,64]{3,2,1,0:T(8,128)S(1)}, s32[]{:S(2)}) async-start(f32[5,16,64,64]{3,2,1,0:T(8,128)} %copy-done.10), calls=%async_computation | async-start | bytes 2097152 | tf_op jit(solution)/shard_map/slice | solution.py:109
  (4 other events, 4.6 us)
where the time goes:
time: 305 us; the launch traced here: 303 us
  local copies, waits for them, and re-layouts  100 us (33%)
  starting transfers between devices  88.2 us (29%)
  other arithmetic  55 us (18%)
  matrix products  36 us (12%)
  waiting for transfers between devices  21.6 us (7%)
    ppermute x8, starting transfers between devices, with_halo(): lax.ppermute(lax.slice_in_dim(block, 0, width, axis=dim), axis, backward)  67.5 us
    gather x8, local copies, waits for them, and re-layouts, place_ghost(): picked = jnp.take(received, mapping, axis=-1)  37.3 us
    ppermute x8, waiting for transfers between devices, from_partner(): return lax.ppermute(block, axis, route)  21.6 us
    ppermute x8, starting transfers between devices, with_halo(): lax.ppermute(lax.slice_in_dim(block, block.shape[dim] - width, None, axis...  15.8 us
    add x2, other arithmetic, tendency(): change = -COURANT * advection + DIFFUSION * laplace  12.8 us
    unnamed x44, local copies, waits for them, and re-layouts  9.34 us
    dot_general x6, matrix products, poisson_solve(): solved = jnp.einsum('ai,mkab->mkib', table_x, solved, precision=precise)  6.89 us
    dot_general x6, matrix products, poisson_solve(): spectral = jnp.einsum('ai,mcij->mcaj', table_x, spectral, precision=precise)  6.88 us
  transfers between devices with their start and end apart: 24, of which 7 were waited for; matrix products, arithmetic and copies ran while one was open for 28% of the time, Pallas kernels for 0%

commit v1 on v0

v1 whole, which is shorter than its diff:
```python
import math

import jax
import jax.numpy as jnp
import numpy as np
from jax import lax
from jax.experimental import pallas as pl
from jax.experimental.pallas import tpu as pltpu
from jax.sharding import PartitionSpec as P

NX = 64
NY = 64
CZ = 16
FIELDS = 5
SECTIONS = 2
ITERS = 3
COURANT = 0.1
DIFFUSION = 0.05
STOICHIOMETRY = 2.0
EXPANSION = 1.0

PLANE = 32
LEVEL = FIELDS * PLANE
HALO = 2
MESH = pl.DeviceIdType.MESH
F32 = jnp.float32
BF16 = jnp.bfloat16


def sine(n):
    i = np.arange(n, dtype=np.float64) + 1.0
    return np.sin(np.pi * i[:, None] * i[None, :] / (n + 1)) * math.sqrt(2.0 / (n + 1))


def eigen(n):
    i = np.arange(n, dtype=np.float64) + 1.0
    return 2.0 - 2.0 * np.cos(np.pi * i / (n + 1))


T_IM = 0
T_Z1 = 512
T_Z2 = 576
T_W = 640
T_SX = 648
T_ROWS = 776
B_Y = 0
B_XF = 128
B_XI = 192
B_ROWS = 256


def tables():
    s16, s64 = sine(CZ), sine(NX)
    tab = np.zeros((T_ROWS, 128))
    modes = eigen(CZ)[:, None, None] + eigen(NX)[None, :, None] + eigen(NY)[None, None, :]
    inv = 1.0 / modes
    tab[T_IM : T_IM + 512] = (
        inv.reshape(8, 2, 64, 64).transpose(0, 2, 1, 3).reshape(512, 128)
    )
    for p in range(8):
        for h in range(2):
            lanes = slice(64 * h, 64 * h + 64)
            for r in range(8):
                tab[T_Z1 + p * 8 + r, lanes] = s16[2 * p + h, 2 * r + h]
                tab[T_Z2 + p * 8 + r, lanes] = s16[2 * p + 1 - h, 2 * r + h]
            tab[T_W + p, lanes] = s16[2 * p + h, 0]
    tab[T_SX : T_SX + 64] = s64[:, 63][:, None]
    tab[T_SX + 64 : T_SX + 128] = s64[:, 0][:, None]
    mat = np.zeros((B_ROWS, 128))
    mat[B_Y : B_Y + 128] = np.kron(np.eye(2), s64)
    order = np.concatenate([np.arange(0, 64, 2), np.arange(1, 64, 2)])
    mat[B_XF : B_XF + 64, :64] = s64[:, order]
    mat[B_XI : B_XI + 64, :64] = s64[order, :]
    mat = mat.astype(np.float32)
    high = mat.astype(jnp.bfloat16)
    low = (mat - high.astype(np.float32)).astype(jnp.bfloat16)
    return tab.astype(np.float32), high, low


S16 = sine(CZ)


def split(v):
    high = v.astype(BF16)
    return high, (v - high.astype(F32)).astype(BF16)


def dot(a, b):
    return jnp.dot(a, b, preferred_element_type=F32)


def dot_right(v, th, tl):
    vh, vl = split(v)
    return dot(vh, th) + (dot(vl, th) + dot(vh, tl))


def dot_left(th, tl, v):
    vh, vl = split(v)
    return dot(th, vh) + (dot(th, vl) + dot(tl, vh))


def kernel(
    state, burn, fmap, tab_h, bh_h, bl_h, out_s, out_p,
    stn, bnn, fld0, fld1, fields, burning, src, ybuf, hat1, hat, prs0, prs1,
    edge, xg, zsend, zrecv, psend, qsend, qrecv, fsend, frecv, tab, bh, bl, idx, outn, outp,
    in_sem, t_sem, out_sem, send_sem, recv_sem,
):
    g = lax.axis_index("grp")
    m = lax.axis_index("mesh")
    n = lax.axis_size("mesh")
    low = lax.rem(m + n - 1, n)
    high = lax.rem(m + 1, n)
    fine = g == 0
    LOW, HIGH, PARTNER = 0, 1, 2
    where_to = ({"mesh": low}, {"mesh": high}, {"grp": 1 - g})

    loads = [
        pltpu.make_async_copy(state.at[f], stn.at[f], in_sem.at[f]) for f in range(FIELDS)
    ]
    loads.append(pltpu.make_async_copy(burn, bnn, in_sem.at[FIELDS]))
    for copy in loads:
        copy.start()
    table_loads = [
        pltpu.make_async_copy(a, b, t_sem.at[i])
        for i, (a, b) in enumerate(((fmap, idx), (tab_h, tab), (bh_h, bh), (bl_h, bl)))
    ]
    for copy in table_loads:
        copy.start()

    barrier = pltpu.get_barrier_semaphore()
    for target in where_to:
        pl.semaphore_signal(barrier, inc=1, device_id=target, device_id_type=MESH)
    pl.semaphore_wait(barrier, 3)

    def remote(exchange, to, a, b):
        slot = exchange * 3 + to
        return pltpu.make_async_remote_copy(
            src_ref=a, dst_ref=b, send_sem=send_sem.at[slot], recv_sem=recv_sem.at[slot],
            device_id=where_to[to], device_id_type=MESH,
        )

    lane = lax.broadcasted_iota(jnp.int32, (PLANE, 128), 1)
    row = lax.broadcasted_iota(jnp.int32, (PLANE, 128), 0)
    half0 = lane < 64
    y_last = (lane == 63) | (lane == 127)
    y_first = (lane == 0) | (lane == 64)
    x_last = (row == PLANE - 1) & (lane >= 64)
    x_first = (row == 0) & half0
    half8 = lax.broadcasted_iota(jnp.int32, (8, 128), 1) < 64
    half64 = lax.broadcasted_iota(jnp.int32, (64, 128), 1) < 64
    sub8 = lax.broadcasted_iota(jnp.int32, (8, 128), 0)

    def swap(v):
        return pltpu.roll(v, 64, 1)

    def rows(start, size):
        return pl.ds(pl.multiple_of(start, 8), size)

    def level(k, f):
        return ((k + HALO) * FIELDS + f) * PLANE

    def to_layers(load, store):
        for b in range(2):
            @pl.loop(0, 4)
            def _(t):
                tiles = jnp.stack(
                    [
                        load(b, pl.ds(pl.multiple_of((t * 8 + i) * 128, 128), 128))
                        for i in range(8)
                    ]
                )
                turned = jnp.swapaxes(tiles, 0, 1)
                for i in range(8):
                    store(b * 8 + i, t * 8, turned[i])

    def to_native(load, store):
        for b in range(2):
            @pl.loop(0, 4)
            def _(t):
                tiles = jnp.stack([load(b * 8 + i, t * 8) for i in range(8)])
                turned = jnp.swapaxes(tiles, 0, 1)
                for i in range(8):
                    store(b, pl.ds(pl.multiple_of((t * 8 + i) * 128, 128), 128), turned[i])

    for f in range(FIELDS):
        loads[f].wait()

        def load_state(b, lanes, f=f):
            return stn[f, b * 8 : b * 8 + 8, lanes]

        def store_state(k, r, v, f=f):
            fld0[rows(level(k, f) + r, 8), :] = v

        to_layers(load_state, store_state)

    def pack_edges():
        for f in range(FIELDS):
            even = edge[pl.ds(f * 16, 8, stride=2), :]
            odd = edge[pl.ds(f * 16 + 1, 8, stride=2), :]
            own = jnp.where(
                fine, jnp.where(half8, swap(even), odd), jnp.where(half8, even, swap(odd))
            )
            yield f, own

    def send_fields(fld, s):
        copies = [
            remote(s * 4, LOW, fld.at[pl.ds(level(0, 0), 2 * LEVEL)],
                   fld.at[pl.ds(level(CZ, 0), 2 * LEVEL)]),
            remote(s * 4, HIGH, fld.at[pl.ds(level(CZ - 2, 0), 2 * LEVEL)],
                   fld.at[pl.ds(level(-2, 0), 2 * LEVEL)]),
            remote(s * 4, PARTNER, fsend.at[s], frecv.at[s]),
        ]
        copies[0].start()
        copies[1].start()
        at = jnp.where(fine, PLANE - 1, 0)
        for k in range(CZ):
            for f in range(FIELDS):
                edge[pl.ds(f * 16 + k, 1), :] = fld[pl.ds(level(k, f) + at, 1), :]
        for f, own in pack_edges():
            fsend[s, f * 8 : f * 8 + 8, :] = own
        copies[2].start()
        return copies

    def gather(plane):
        index = idx[...]
        column = index & 127
        block = index >> 7
        out = jnp.zeros((8, 128), F32)
        for r in range(8):
            one = jnp.broadcast_to(plane[r : r + 1, :], (8, 128))
            out = jnp.where(block == r, jnp.take_along_axis(one, column, axis=1), out)
        return out

    def spread(ghost, base):
        other = swap(ghost)
        xg[pl.ds(base, 8, stride=2), :] = jnp.where(half8, ghost, other)
        xg[pl.ds(base + 1, 8, stride=2), :] = jnp.where(half8, other, ghost)

    def x_sides(v, ghost):
        ghost = jnp.broadcast_to(ghost, (PLANE, 128))
        turned = swap(v)
        up = pltpu.roll(turned, PLANE - 1, 0)
        down = pltpu.roll(turned, 1, 0)
        zero = jnp.zeros_like(ghost)
        up = jnp.where(x_last, jnp.where(fine, ghost, zero), up)
        down = jnp.where(x_first, jnp.where(fine, zero, ghost), down)
        return jnp.where(half0, turned, up), jnp.where(half0, down, turned)

    def y_sides(v):
        north = jnp.where(y_last, 0.0, pltpu.roll(v, 127, 1))
        south = jnp.where(y_first, 0.0, pltpu.roll(v, 1, 1))
        return north, south

    def tendency_plane(fld, k, finish):
        c = [fld[rows(level(k, f), PLANE), :] for f in range(FIELDS)]
        reaction = burning[rows(k * PLANE, PLANE), :] * c[3] * c[4]
        source = EXPANSION * reaction
        for f in range(FIELDS):
            above = fld[rows(level(k + 1, f), PLANE), :]
            below = fld[rows(level(k - 1, f), PLANE), :]
            above2 = fld[rows(level(k + 2, f), PLANE), :]
            below2 = fld[rows(level(k - 2, f), PLANE), :]
            east, west = x_sides(c[f], xg[pl.ds(f * 16 + k, 1), :])
            north, south = y_sides(c[f])
            gx = 0.5 * (east - west)
            gy = 0.5 * (north - south)
            dz = above - below
            gz = (2.0 / 3.0) * dz - (1.0 / 12.0) * (above2 - below2)
            lap = (east + west) + (north + south) + (above + below) - 6.0 * c[f]
            adv = c[0] * gx + c[1] * gy + c[2] * gz
            change = DIFFUSION * lap - COURANT * adv
            if f == 0:
                source = source - gx
            elif f == 1:
                source = source - gy
            elif f == 2:
                source = source - 0.5 * dz
            elif f == 3:
                change = change - reaction
            else:
                change = change - STOICHIOMETRY * reaction
            finish(k, f, c[f], change)
        src[rows(k * PLANE, PLANE), :] = source

    def z_forward(into):
        @pl.loop(0, 4)
        def _(t):
            v = [src[rows(k * PLANE + t * 8, 8), :] for k in range(CZ)]
            even = [v[k] + v[15 - k] for k in range(8)]
            odd = [v[k] - v[15 - k] for k in range(8)]
            for c in range(CZ):
                part = odd if c % 2 else even
                total = part[0] * F32(S16[c, 0])
                for k in range(1, 8):
                    total = total + part[k] * F32(S16[c, k])
                into[rows(c * PLANE + t * 8, 8), :] = total

    def z_inverse(spec, into, base):
        @pl.loop(0, 4)
        def _(t):
            v = [spec[rows(c * PLANE + t * 8, 8), :] for c in range(CZ)]
            for k in range(8):
                even = v[0] * F32(S16[0, k])
                odd = v[1] * F32(S16[1, k])
                for c in range(1, 8):
                    even = even + v[2 * c] * F32(S16[2 * c, k])
                    odd = odd + v[2 * c + 1] * F32(S16[2 * c + 1, k])
                into[rows(base + k * PLANE + t * 8, 8), :] = even + odd
                into[rows(base + (15 - k) * PLANE + t * 8, 8), :] = even - odd

    def y_matrix():
        return bh[B_Y : B_Y + 128, :], bl[B_Y : B_Y + 128, :]

    def y_transform(v):
        return dot_right(v, *y_matrix())

    def x_forward(a, b):
        even = jnp.where(half0, a, swap(b))
        odd = jnp.where(half0, swap(a), b)
        v = jnp.concatenate([even, odd], axis=0)
        return dot_left(bh[B_XF : B_XF + 64, :64], bl[B_XF : B_XF + 64, :64], v)

    def x_inverse(v):
        v = dot_left(bh[B_XI : B_XI + 64, :64], bl[B_XI : B_XI + 64, :64], v)
        even, odd = v[:PLANE], v[PLANE:]
        return jnp.where(half0, even, swap(odd)), jnp.where(half0, swap(even), odd)

    def z_plane(v):
        other = swap(v)
        out = jnp.zeros((8, 128), F32)
        for p in range(8):
            out = out + tab[T_Z1 + p * 8 : T_Z1 + p * 8 + 8, :] * v[p : p + 1, :]
            out = out + tab[T_Z2 + p * 8 : T_Z2 + p * 8 + 8, :] * other[p : p + 1, :]
        return out

    def side_x():
        return tab[rows(T_SX + g * 64, 64), :]

    def interfaces(spec):
        sx = side_x()
        acc = jnp.zeros((64, 128), F32)
        plane = []
        for p in range(8):
            v = spec[p * 64 : p * 64 + 64, :]
            acc = acc + tab[T_W + p : T_W + p + 1, :] * v
            plane.append(jnp.sum(sx * v, axis=0, keepdims=True))
        other = swap(acc)
        first = acc + other
        last = jnp.where(half64, acc - other, other - acc)
        plane = z_plane(y_transform(jnp.concatenate(plane, axis=0)))
        return first, last, plane

    def narrow(v):
        return jnp.where(half0, v[:PLANE], v[PLANE:])

    def widen(v):
        other = swap(v)
        return jnp.concatenate(
            [jnp.where(half0, v, other), jnp.where(half0, other, v)], axis=0
        )

    at_low = m > 0
    at_high = m < n - 1
    pending = []

    def solve(s, prs):
        z_forward(ybuf)
        ybuf[...] = y_transform(ybuf[...])
        for p in range(8):
            v = x_forward(
                ybuf[2 * p * PLANE : (2 * p + 1) * PLANE, :],
                ybuf[(2 * p + 1) * PLANE : (2 * p + 2) * PLANE, :],
            )
            hat1[p * 64 : p * 64 + 64, :] = v * tab[T_IM + p * 64 : T_IM + p * 64 + 64, :]
        spec = hat1
        for e in range(ITERS - 1):
            at = s * 2 + e
            first, last, plane = interfaces(spec)
            qsend[s * 3 + e] = plane
            zsend[at * 2] = narrow(first)
            zsend[at * 2 + 1] = narrow(last)
            copies = [
                remote(s * 4 + 1 + e, LOW, zsend.at[at * 2], zrecv.at[at * 2 + 1]),
                remote(s * 4 + 1 + e, HIGH, zsend.at[at * 2 + 1], zrecv.at[at * 2]),
                remote(s * 4 + 1 + e, PARTNER, qsend.at[s * 3 + e], qrecv.at[s * 3 + e]),
            ]
            for copy in copies:
                copy.start()
            copies[2].wait_recv()
            ghost = y_transform(z_plane(gather(qrecv[s * 3 + e])))
            copies[0].wait_recv()
            copies[1].wait_recv()
            pending.extend(copies)
            below = widen(jnp.where(at_low, zrecv[at * 2], 0.0))
            above = widen(jnp.where(at_high, zrecv[at * 2 + 1], 0.0))
            both = below + jnp.where(half64, above, -above)
            sx = side_x()
            for p in range(8):
                extra = tab[T_W + p : T_W + p + 1, :] * both + sx * ghost[p : p + 1, :]
                hat[p * 64 : p * 64 + 64, :] = (
                    hat1[p * 64 : p * 64 + 64, :]
                    + extra * tab[T_IM + p * 64 : T_IM + p * 64 + 64, :]
                )
            spec = hat
        e = ITERS - 1
        first, last, plane = interfaces(hat)
        qsend[s * 3 + e] = plane
        a, b = x_inverse(jnp.where(half64, first, last))
        psend[s * 2] = y_transform(a)
        psend[s * 2 + 1] = y_transform(b)
        copies = [
            remote(s * 4 + 3, LOW, psend.at[s * 2], prs.at[pl.ds((CZ + 1) * PLANE, PLANE)]),
            remote(s * 4 + 3, HIGH, psend.at[s * 2 + 1], prs.at[pl.ds(0, PLANE)]),
            remote(s * 4 + 3, PARTNER, qsend.at[s * 3 + e], qrecv.at[s * 3 + e]),
        ]
        for copy in copies:
            copy.start()
        pending.extend(copies)
        for p in range(8):
            a, b = x_inverse(hat[p * 64 : p * 64 + 64, :])
            ybuf[2 * p * PLANE : (2 * p + 1) * PLANE, :] = a
            ybuf[(2 * p + 1) * PLANE : (2 * p + 2) * PLANE, :] = b
        ybuf[...] = y_transform(ybuf[...])
        z_inverse(ybuf, prs, PLANE)
        copies[2].wait_recv()
        spread(gather(qrecv[s * 3 + e]), 0)
        copies[0].wait_recv()
        copies[1].wait_recv()

        @pl.when(jnp.logical_not(at_low))
        def _():
            prs[0:PLANE, :] = jnp.zeros((PLANE, 128), F32)

        @pl.when(jnp.logical_not(at_high))
        def _():
            prs[(CZ + 1) * PLANE : (CZ + 2) * PLANE, :] = jnp.zeros((PLANE, 128), F32)

    def correct(prs, into, base):
        @pl.loop(0, CZ)
        def _(k):
            p = prs[rows((k + 1) * PLANE, PLANE), :]
            above = prs[rows((k + 2) * PLANE, PLANE), :]
            below = prs[rows(k * PLANE, PLANE), :]
            east, west = x_sides(p, xg[pl.ds(k, 1), :])
            north, south = y_sides(p)
            for f, (a, b) in enumerate(((east, west), (north, south), (above, below))):
                at = rows(base + (k * FIELDS + f) * PLANE, PLANE)
                into[at, :] = into[at, :] - 0.5 * (a - b)

    for s in range(SECTIONS):
        fld = (fld0, fld1)[s]
        prs = (prs0, prs1)[s]
        copies = send_fields(fld, s)
        pending.extend(copies)
        if s == 0:
            loads[FIELDS].wait()

            def load_burn(b, lanes):
                return bnn[b * 8 : b * 8 + 8, lanes]

            def store_burn(k, r, v):
                burning[rows(k * PLANE + r, 8), :] = v

            to_layers(load_burn, store_burn)
            for copy in table_loads:
                copy.wait()

            def finish(k, f, c, change):
                fld1[rows(level(k, f), PLANE), :] = c + change
        else:

            def finish(k, f, c, change):
                start = fld0[rows(level(k, f), PLANE), :]
                fields[rows((k * FIELDS + f) * PLANE, PLANE), :] = 0.5 * (start + c + change)

        copies[2].wait_recv()
        for f in range(FIELDS):
            spread(gather(frecv[s, f * 8 : f * 8 + 8, :]), f * 16)

        @pl.loop(2, CZ - 2)
        def _(k, fld=fld, finish=finish):
            tendency_plane(fld, k, finish)

        copies[0].wait_recv()
        copies[1].wait_recv()

        @pl.when(jnp.logical_not(at_low))
        def _(fld=fld):
            fld[0 : 2 * LEVEL, :] = jnp.zeros((2 * LEVEL, 128), F32)

        @pl.when(jnp.logical_not(at_high))
        def _(fld=fld):
            fld[level(CZ, 0) : level(CZ + 2, 0), :] = jnp.zeros((2 * LEVEL, 128), F32)

        @pl.loop(0, 4)
        def _(i, fld=fld, finish=finish):
            tendency_plane(fld, i + (CZ - 4) * (i // 2), finish)

        solve(s, prs)
        if s == 0:
            correct(prs, fld1, level(0, 0))
        else:
            correct(prs, fields, 0)

    def load_field(k, r, f):
        return fields[rows((k * FIELDS + f) * PLANE + r, 8), :]

    stores = []
    for f in range(FIELDS):
        def store_field(b, lanes, v, f=f):
            outn[f, b * 8 : b * 8 + 8, lanes] = v

        to_native(lambda k, r, f=f: load_field(k, r, f), store_field)
        stores.append(pltpu.make_async_copy(outn.at[f], out_s.at[f], out_sem.at[f]))
        stores[-1].start()

    def store_head(b, lanes, v):
        outp[b * 8 : b * 8 + 8, lanes] = v

    to_native(lambda k, r: prs1[rows((k + 1) * PLANE + r, 8), :], store_head)
    stores.append(pltpu.make_async_copy(outp, out_p, out_sem.at[FIELDS]))
    stores[-1].start()
    for copy in pending:
        copy.wait_send()
    for copy in stores:
        copy.wait()


def step(state, burn, fmap):
    anywhere = pl.BlockSpec(memory_space=pl.ANY)
    tab, bh, bl = tables()
    vm = pltpu.VMEM
    layers = (CZ + 2 * HALO) * LEVEL
    return pl.pallas_call(
        kernel,
        out_shape=(
            jax.ShapeDtypeStruct((FIELDS, CZ, NX * NY), F32),
            jax.ShapeDtypeStruct((CZ, NX * NY), F32),
        ),
        in_specs=[anywhere] * 6,
        out_specs=(anywhere, anywhere),
        scratch_shapes=[
            vm((FIELDS, CZ, NX * NY), F32),
            vm((CZ, NX * NY), F32),
            vm((layers, 128), F32),
            vm((layers, 128), F32),
            vm((CZ * LEVEL, 128), F32),
            vm((CZ * PLANE, 128), F32),
            vm((CZ * PLANE, 128), F32),
            vm((CZ * PLANE, 128), F32),
            vm((CZ * PLANE, 128), F32),
            vm((CZ * PLANE, 128), F32),
            vm(((CZ + 2) * PLANE, 128), F32),
            vm(((CZ + 2) * PLANE, 128), F32),
            vm((FIELDS * 16, 128), F32),
            vm((FIELDS * 16, 128), F32),
            vm((8, PLANE, 128), F32),
            vm((8, PLANE, 128), F32),
            vm((4, PLANE, 128), F32),
            vm((6, 8, 128), F32),
            vm((6, 8, 128), F32),
            vm((2, FIELDS * 8, 128), F32),
            vm((2, FIELDS * 8, 128), F32),
            vm((T_ROWS, 128), F32),
            vm((B_ROWS, 128), BF16),
            vm((B_ROWS, 128), BF16),
            vm((8, 128), jnp.int32),
            vm((FIELDS, CZ, NX * NY), F32),
            vm((CZ, NX * NY), F32),
            pltpu.SemaphoreType.DMA((FIELDS + 1,)),
            pltpu.SemaphoreType.DMA((4,)),
            pltpu.SemaphoreType.DMA((FIELDS + 1,)),
            pltpu.SemaphoreType.DMA((24,)),
            pltpu.SemaphoreType.DMA((24,)),
        ],
        compiler_params=pltpu.CompilerParams(
            collective_id=0, has_side_effects=True, vmem_limit_bytes=40 << 20
        ),
        name="fire_step",
    )(state, burn, fmap, jnp.asarray(tab), jnp.asarray(bh), jnp.asarray(bl))


def shards(state, burn_rate, face_map):
    fields, head = step(state[0], burn_rate[0], face_map.reshape(8, 128))
    return fields[None], head[None]


def solution(mesh):
    placed = (P("grp", None, "mesh", None), P("grp", "mesh", None), P("grp", "mesh", None))
    return jax.shard_map(
        shards,
        mesh=mesh,
        in_specs=placed,
        out_specs=(P("grp", None, "mesh", None), P("grp", "mesh", None)),
        check_vma=False,
    )
```

time: 305 us -> 72.8 us (0.24)
  the two profiles are of different devices: /device:TPU:128 before, /device:TPU:8 now
where the time goes in v1:
time: 72.8 us; the launch traced here: 72.5 us
  Pallas kernels  64.5 us (89%)
  local copies, waits for them, and re-layouts  7.38 us (10%)
    pallas_call x1, Pallas kernels, step(): pl.pallas_call(kernel, out_shape=(jax.ShapeDtypeStruct((FIELDS, CZ, NX *...  64.5 us
    unnamed x14, local copies, waits for them, and re-layouts  7.38 us

profile of v1, /device:TPU:8, one launch (start us, length us, event | category | flops | bytes accessed | tf_op | source)
XLA Modules:
  0.0 72.5 jit_solution(2339835109071420035)
XLA Ops:
  0.6 0.0 copy-start
  0.6 1.3 %copy-done = f32[1,5,16,4096]{3,2,1,0:T(8,128)S(1)} copy-done((f32[1,5,16,4096]{3,2,1,0:T(8,128)S(1)}, f32[1,5,16,4096]{3,2,1,0:T(8,128)}, u32[]{:S(2)}) %copy-start) | copy-done | bytes 1310744
  1.9 0.0 copy-start.1
  1.9 1.0 %copy-done.1 = f32[776,128]{1,0:T(8,128)S(1)} copy-done((f32[776,128]{1,0:T(8,128)S(1)}, f32[776,128]{1,0:T(8,128)}, u32[]{:S(2)}) %copy-start.1) | copy-done | bytes 397336
  2.9 0.0 copy-start.2
  2.9 0.9 %copy-done.2 = f32[1,16,4096]{2,1,0:T(8,128)S(1)} copy-done((f32[1,16,4096]{2,1,0:T(8,128)S(1)}, f32[1,16,4096]{2,1,0:T(8,128)}, u32[]{:S(2)}) %copy-start.2) | copy-done | bytes 262168
  3.9 0.0 copy-start.3
  3.9 0.8 %copy-done.3 = bf16[256,128]{1,0:T(8,128)(2,1)S(1)} copy-done((bf16[256,128]{1,0:T(8,128)(2,1)S(1)}, bf16[256,128]{1,0:T(8,128)(2,1)}, u32[]{:S(2)}) %copy-start.3) | copy-done | bytes 65560
  4.7 0.0 copy-start.4
  4.7 0.8 %copy-done.4 = bf16[256,128]{1,0:T(8,128)(2,1)S(1)} copy-done((bf16[256,128]{1,0:T(8,128)(2,1)S(1)}, bf16[256,128]{1,0:T(8,128)(2,1)}, u32[]{:S(2)}) %copy-start.4) | copy-done | bytes 65560
  5.6 0.0 copy-start.5
  5.6 0.7 copy-done.5
  6.3 64.5 %fire_step.1 = (f32[5,16,4096]{2,1,0:T(8,128)S(1)}, f32[16,4096]{1,0:T(8,128)S(1)}) custom-call(f32[5,16,4096]{2,1,0:T(8,128)S(1)} %bitcast.6, f32[16,4096]{1,0:T(8,128)S(1)} %bitcast.8, s32[8,128]{1,0:T(8,128)S(1)} %bitcast.9, f32[776,128]{1,0:T(8,128)S(1)} %copy-done.1, bf16[256,128]{1,0:T(8,128)(2,1)S(1)} %copy-done.4, bf16[256,128]{1,0:T(8,128)(2,1)S(1)} %copy-done.3), custom_call_target="tpu_custom_call" | custom-call | tf_op jit(solution)/shard_map/fire_step/pallas_call | solution.py:534
  70.8 1.1 %copy.10 = f32[1,5,16,4096]{3,2,1,0:T(8,128)} copy(f32[1,5,16,4096]{3,2,1,0:T(8,128)S(1)} %bitcast.5) | data formatting | bytes 2621440
  71.8 0.7 copy.11
Async XLA Ops:
  0.6 1.3 %copy-start = (f32[1,5,16,4096]{3,2,1,0:T(8,128)S(1)}, f32[1,5,16,4096]{3,2,1,0:T(8,128)}, u32[]{:S(2)}) copy-start(f32[1,5,16,4096]{3,2,1,0:T(8,128)} %param.6) | copy-start | bytes 3932164
  1.9 1.0 %copy-start.1 = (f32[776,128]{1,0:T(8,128)S(1)}, f32[776,128]{1,0:T(8,128)}, u32[]{:S(2)}) copy-start(f32[776,128]{1,0:T(8,128)} %constant.6.clone.tab_h) | copy-start | bytes 1191940
  2.9 0.9 %copy-start.2 = (f32[1,16,4096]{2,1,0:T(8,128)S(1)}, f32[1,16,4096]{2,1,0:T(8,128)}, u32[]{:S(2)}) copy-start(f32[1,16,4096]{2,1,0:T(8,128)} %param.7) | copy-start | bytes 786436
  3.9 0.8 %copy-start.3 = (bf16[256,128]{1,0:T(8,128)(2,1)S(1)}, bf16[256,128]{1,0:T(8,128)(2,1)}, u32[]{:S(2)}) copy-start(bf16[256,128]{1,0:T(8,128)(2,1)} %constant.8.clone.bl_h) | copy-start | bytes 196612
  4.7 0.8 %copy-start.4 = (bf16[256,128]{1,0:T(8,128)(2,1)S(1)}, bf16[256,128]{1,0:T(8,128)(2,1)}, u32[]{:S(2)}) copy-start(bf16[256,128]{1,0:T(8,128)(2,1)} %constant.7.clone.bh_h) | copy-start | bytes 196612
  5.6 0.7 copy-start.5

commit v2 on v1

v2 whole, which is shorter than its diff:
```python
import math

import jax
import jax.numpy as jnp
import numpy as np
from jax import lax
from jax.experimental import pallas as pl
from jax.experimental.pallas import tpu as pltpu
from jax.sharding import PartitionSpec as P

NX = 64
NY = 64
CZ = 16
FIELDS = 5
SECTIONS = 2
ITERS = 3
COURANT = 0.1
DIFFUSION = 0.05
STOICHIOMETRY = 2.0
EXPANSION = 1.0

PLANE = 32
LEVEL = FIELDS * PLANE
HALO = 2
MESH = pl.DeviceIdType.MESH
F32 = jnp.float32
BF16 = jnp.bfloat16


def sine(n):
    i = np.arange(n, dtype=np.float64) + 1.0
    return np.sin(np.pi * i[:, None] * i[None, :] / (n + 1)) * math.sqrt(2.0 / (n + 1))


def eigen(n):
    i = np.arange(n, dtype=np.float64) + 1.0
    return 2.0 - 2.0 * np.cos(np.pi * i / (n + 1))


T_IM = 0
T_Z1 = 512
T_Z2 = 576
T_W = 640
T_GAMMA = 664
T_ALPHA = 672
T_SX = 736
T_SX2 = 864
T_ROWS = 992
B_Y = 0
B_XF = 128
B_XI = 192
B_ROWS = 256


def tables():
    s16, s64 = sine(CZ), sine(NX)
    tab = np.zeros((T_ROWS, 128))
    modes = eigen(CZ)[:, None, None] + eigen(NX)[None, :, None] + eigen(NY)[None, None, :]
    inv = 1.0 / modes
    tab[T_IM : T_IM + 512] = (
        inv.reshape(8, 2, 64, 64).transpose(0, 2, 1, 3).reshape(512, 128)
    )
    for p in range(8):
        for h in range(2):
            lanes = slice(64 * h, 64 * h + 64)
            for r in range(8):
                tab[T_Z1 + p * 8 + r, lanes] = s16[2 * p + h, 2 * r + h]
                tab[T_Z2 + p * 8 + r, lanes] = s16[2 * p + 1 - h, 2 * r + h]
            for k in range(3):
                tab[T_W + 8 * k + p, lanes] = s16[2 * p + h, k]
    for at, places in ((T_SX, (63, 0)), (T_SX2, (62, 1))):
        for side, place in enumerate(places):
            tab[at + 64 * side : at + 64 * side + 64] = s64[:, place][:, None]
    packed = tab[T_IM : T_IM + 512].reshape(8, 64, 128)
    tab[T_ALPHA : T_ALPHA + 64] = (packed * tab[T_W : T_W + 8, None, :] ** 2).sum(0)
    tab[T_GAMMA : T_GAMMA + 8] = (packed * tab[None, T_SX : T_SX + 64] ** 2).sum(1)
    mat = np.zeros((B_ROWS, 128))
    mat[B_Y : B_Y + 128] = np.kron(np.eye(2), s64)
    order = np.concatenate([np.arange(0, 64, 2), np.arange(1, 64, 2)])
    mat[B_XF : B_XF + 64, :64] = s64[:, order]
    mat[B_XI : B_XI + 64, :64] = s64[order, :]
    mat = mat.astype(np.float32)
    high = mat.astype(jnp.bfloat16)
    low = (mat - high.astype(np.float32)).astype(jnp.bfloat16)
    return tab.astype(np.float32), high, low


S16 = sine(CZ)


def split(v):
    high = v.astype(BF16)
    return high, (v - high.astype(F32)).astype(BF16)


def dot(a, b):
    return jnp.dot(a, b, preferred_element_type=F32)


def dot_right(v, th, tl):
    vh, vl = split(v)
    return dot(vh, th) + (dot(vl, th) + dot(vh, tl))


def dot_left(th, tl, v):
    vh, vl = split(v)
    return dot(th, vh) + (dot(th, vl) + dot(tl, vh))


def kernel(
    state, burn, fmap, tab_h, bh_h, bl_h, out_s, out_p,
    stn, bnn, fld0, fld1, fields, burning, src, ybuf, hat1, hat, prs, resp,
    edge, xg, zsend, zrecv, psend, qsend, qrecv, fsend, frecv, psel, tab, bh, bl, idx,
    in_sem, t_sem, send_sem, recv_sem,
):
    g = lax.axis_index("grp")
    m = lax.axis_index("mesh")
    n = lax.axis_size("mesh")
    fine = g == 0
    LOW, HIGH, PARTNER, LOW2, HIGH2, DLOW, DHIGH = range(7)
    back = (HIGH, LOW, PARTNER, HIGH2, LOW2, DHIGH, DLOW)
    has_low, has_high = m > 0, m < n - 1
    exists = (has_low, has_high, None, m > 1, m < n - 2, has_low, has_high)
    steps = (-1, 1, 0, -2, 2, -1, 1)
    where_to = [
        {"grp": 1 - g if to in (PARTNER, DLOW, DHIGH) else g, "mesh": lax.rem(m + n + steps[to], n)}
        for to in range(7)
    ]
    count = 1
    for to in range(7):
        if exists[to] is not None:
            count = count + exists[to].astype(jnp.int32)

    def guarded(condition, action):
        if condition is None:
            action()
        else:
            pl.when(condition)(action)

    loads = [
        pltpu.make_async_copy(state.at[f], stn.at[f], in_sem.at[f]) for f in range(FIELDS)
    ]
    loads.append(pltpu.make_async_copy(burn, bnn, in_sem.at[FIELDS]))
    for copy in loads:
        copy.start()
    table_loads = [
        pltpu.make_async_copy(a, b, t_sem.at[i])
        for i, (a, b) in enumerate(((fmap, idx.at[0]), (tab_h, tab), (bh_h, bh), (bl_h, bl)))
    ]
    for copy in table_loads:
        copy.start()

    def clear(ref, start, size):
        ref[start : start + size, :] = jnp.zeros((size, 128), F32)

    @pl.when(jnp.logical_not(has_low))
    def _():
        clear(fld0, 0, 2 * LEVEL)
        clear(fld1, 0, 2 * LEVEL)
        for s in range(SECTIONS):
            clear(prs.at[s], 0, 3 * PLANE)
            for part in (1, 4):
                clear(zrecv.at[s, part], 0, PLANE + 8)
            clear(qrecv.at[s, 1], 0, 8)

    @pl.when(jnp.logical_not(has_high))
    def _():
        clear(fld0, (CZ + 2) * LEVEL, 2 * LEVEL)
        clear(fld1, (CZ + 2) * LEVEL, 2 * LEVEL)
        for s in range(SECTIONS):
            clear(prs.at[s], (CZ + 3) * PLANE, 3 * PLANE)
            for part in (0, 5):
                clear(zrecv.at[s, part], 0, PLANE + 8)
            clear(qrecv.at[s, 2], 0, 8)

    @pl.when(m < 2)
    def _():
        for s in range(SECTIONS):
            clear(zrecv.at[s, 3], 0, PLANE + 8)

    @pl.when(m > n - 3)
    def _():
        for s in range(SECTIONS):
            clear(zrecv.at[s, 2], 0, PLANE + 8)

    barrier = pltpu.get_barrier_semaphore()
    for to in range(7):
        guarded(
            exists[to],
            lambda to=to: pl.semaphore_signal(
                barrier, inc=1, device_id=where_to[to], device_id_type=MESH
            ),
        )
    pl.semaphore_wait(barrier, count)

    messages = []

    class Message:
        def __init__(self, to, a, b):
            slot = len(messages)
            messages.append(self)
            self.to = to
            self.copy = pltpu.make_async_remote_copy(
                src_ref=a, dst_ref=b, send_sem=send_sem.at[slot], recv_sem=recv_sem.at[slot],
                device_id=where_to[to], device_id_type=MESH,
            )
            self.sent = False

        def start(self):
            guarded(exists[self.to], self.copy.start)

        def wait_recv(self):
            guarded(exists[back[self.to]], self.copy.wait_recv)

        def wait_send(self):
            if not self.sent:
                self.sent = True
                guarded(exists[self.to], self.copy.wait_send)

    lane = lax.broadcasted_iota(jnp.int32, (PLANE, 128), 1)
    row = lax.broadcasted_iota(jnp.int32, (PLANE, 128), 0)
    half0 = lane < 64
    y_last = (lane == 63) | (lane == 127)
    y_first = (lane == 0) | (lane == 64)
    x_last = (row == PLANE - 1) & (lane >= 64)
    x_first = (row == 0) & half0
    half8 = lax.broadcasted_iota(jnp.int32, (8, 128), 1) < 64
    half64 = lax.broadcasted_iota(jnp.int32, (64, 128), 1) < 64
    sub8 = lax.broadcasted_iota(jnp.int32, (8, 128), 0)

    def swap(v):
        return pltpu.roll(v, 64, 1)

    def rows(start, size):
        return pl.ds(pl.multiple_of(start, 8), size)

    def level(k, f):
        return ((k + HALO) * FIELDS + f) * PLANE

    def to_layers(load, store):
        for b in range(2):
            @pl.loop(0, 4)
            def _(t):
                tiles = jnp.stack(
                    [
                        load(b, pl.ds(pl.multiple_of((t * 8 + i) * 128, 128), 128))
                        for i in range(8)
                    ]
                )
                turned = jnp.swapaxes(tiles, 0, 1)
                for i in range(8):
                    store(b * 8 + i, t * 8, turned[i])

    def to_native(load, store):
        for b in range(2):
            @pl.loop(0, 4)
            def _(t):
                tiles = jnp.stack([load(b * 8 + i, t * 8) for i in range(8)])
                turned = jnp.swapaxes(tiles, 0, 1)
                for i in range(8):
                    store(b, pl.ds(pl.multiple_of((t * 8 + i) * 128, 128), 128), turned[i])

    for f in range(FIELDS):
        loads[f].wait()

        def load_state(b, lanes, f=f):
            return stn[f, b * 8 : b * 8 + 8, lanes]

        def store_state(k, r, v, f=f):
            fld0[rows(level(k, f) + r, 8), :] = v

        to_layers(load_state, store_state)

    def pack_edges():
        for f in range(FIELDS):
            even = edge[pl.ds(f * 16, 8, stride=2), :]
            odd = edge[pl.ds(f * 16 + 1, 8, stride=2), :]
            own = jnp.where(
                fine, jnp.where(half8, swap(even), odd), jnp.where(half8, even, swap(odd))
            )
            yield f, own

    def send_fields(fld, s):
        copies = [
            Message(LOW, fld.at[pl.ds(level(0, 0), 2 * LEVEL)],
                    fld.at[pl.ds(level(CZ, 0), 2 * LEVEL)]),
            Message(HIGH, fld.at[pl.ds(level(CZ - 2, 0), 2 * LEVEL)],
                    fld.at[pl.ds(level(-2, 0), 2 * LEVEL)]),
            Message(PARTNER, fsend.at[s], frecv.at[s]),
        ]
        copies[0].start()
        copies[1].start()
        at = jnp.where(fine, PLANE - 1, 0)
        for k in range(CZ):
            for f in range(FIELDS):
                edge[pl.ds(f * 16 + k, 1), :] = fld[pl.ds(level(k, f) + at, 1), :]
        for f, own in pack_edges():
            fsend[s, f * 8 : f * 8 + 8, :] = own
        copies[2].start()
        return copies

    def gather(plane, who=0):
        index = idx[who]
        column = index & 127
        block = index >> 7
        out = jnp.zeros((8, 128), F32)
        for r in range(8):
            one = jnp.broadcast_to(plane[r : r + 1, :], (8, 128))
            out = jnp.where(block == r, jnp.take_along_axis(one, column, axis=1), out)
        return out

    def spread(ghost, base):
        other = swap(ghost)
        xg[pl.ds(base, 8, stride=2), :] = jnp.where(half8, ghost, other)
        xg[pl.ds(base + 1, 8, stride=2), :] = jnp.where(half8, other, ghost)

    def x_sides(v, ghost):
        ghost = jnp.broadcast_to(ghost, (PLANE, 128))
        turned = swap(v)
        up = pltpu.roll(turned, PLANE - 1, 0)
        down = pltpu.roll(turned, 1, 0)
        zero = jnp.zeros_like(ghost)
        up = jnp.where(x_last, jnp.where(fine, ghost, zero), up)
        down = jnp.where(x_first, jnp.where(fine, zero, ghost), down)
        return jnp.where(half0, turned, up), jnp.where(half0, down, turned)

    def y_sides(v):
        north = jnp.where(y_last, 0.0, pltpu.roll(v, 127, 1))
        south = jnp.where(y_first, 0.0, pltpu.roll(v, 1, 1))
        return north, south

    XG = 48

    def tendency_plane(fld, k, finish):
        c = [fld[rows(level(k, f), PLANE), :] for f in range(FIELDS)]
        reaction = burning[rows(k * PLANE, PLANE), :] * c[3] * c[4]
        source = EXPANSION * reaction
        for f in range(FIELDS):
            above = fld[rows(level(k + 1, f), PLANE), :]
            below = fld[rows(level(k - 1, f), PLANE), :]
            above2 = fld[rows(level(k + 2, f), PLANE), :]
            below2 = fld[rows(level(k - 2, f), PLANE), :]
            east, west = x_sides(c[f], xg[pl.ds(XG + f * 16 + k, 1), :])
            north, south = y_sides(c[f])
            gx = 0.5 * (east - west)
            gy = 0.5 * (north - south)
            dz = above - below
            gz = (2.0 / 3.0) * dz - (1.0 / 12.0) * (above2 - below2)
            lap = (east + west) + (north + south) + (above + below) - 6.0 * c[f]
            adv = c[0] * gx + c[1] * gy + c[2] * gz
            change = DIFFUSION * lap - COURANT * adv
            if f == 0:
                source = source - gx
            elif f == 1:
                source = source - gy
            elif f == 2:
                source = source - 0.5 * dz
            elif f == 3:
                change = change - reaction
            else:
                change = change - STOICHIOMETRY * reaction
            finish(k, f, c[f], change)
        src[rows(k * PLANE, PLANE), :] = source

    def z_forward(into):
        @pl.loop(0, 4)
        def _(t):
            v = [src[rows(k * PLANE + t * 8, 8), :] for k in range(CZ)]
            even = [v[k] + v[15 - k] for k in range(8)]
            odd = [v[k] - v[15 - k] for k in range(8)]
            for c in range(CZ):
                part = odd if c % 2 else even
                total = part[0] * F32(S16[c, 0])
                for k in range(1, 8):
                    total = total + part[k] * F32(S16[c, k])
                into[rows(c * PLANE + t * 8, 8), :] = total

    def z_inverse(spec, into, base):
        @pl.loop(0, 4)
        def _(t):
            v = [spec[rows(c * PLANE + t * 8, 8), :] for c in range(CZ)]
            for k in range(8):
                even = v[0] * F32(S16[0, k])
                odd = v[1] * F32(S16[1, k])
                for c in range(1, 8):
                    even = even + v[2 * c] * F32(S16[2 * c, k])
                    odd = odd + v[2 * c + 1] * F32(S16[2 * c + 1, k])
                into[rows(base + k * PLANE + t * 8, 8), :] = even + odd
                into[rows(base + (15 - k) * PLANE + t * 8, 8), :] = even - odd

    def y_matrix():
        return bh[B_Y : B_Y + 128, :], bl[B_Y : B_Y + 128, :]

    def y_transform(v):
        return dot_right(v, *y_matrix())

    def x_forward(a, b):
        even = jnp.where(half0, a, swap(b))
        odd = jnp.where(half0, swap(a), b)
        v = jnp.concatenate([even, odd], axis=0)
        return dot_left(bh[B_XF : B_XF + 64, :64], bl[B_XF : B_XF + 64, :64], v)

    def x_inverse(v):
        v = dot_left(bh[B_XI : B_XI + 64, :64], bl[B_XI : B_XI + 64, :64], v)
        even, odd = v[:PLANE], v[PLANE:]
        return jnp.where(half0, even, swap(odd)), jnp.where(half0, swap(even), odd)

    def z_plane(v):
        other = swap(v)
        out = jnp.zeros((8, 128), F32)
        for p in range(8):
            out = out + tab[T_Z1 + p * 8 : T_Z1 + p * 8 + 8, :] * v[p : p + 1, :]
            out = out + tab[T_Z2 + p * 8 : T_Z2 + p * 8 + 8, :] * other[p : p + 1, :]
        return out

    def side_x(at=T_SX):
        return tab[rows(at + g * 64, 64), :]

    def weight(k, p):
        return tab[T_W + 8 * k + p : T_W + 8 * k + p + 1, :]

    def modes(p):
        return tab[T_IM + p * 64 : T_IM + p * 64 + 64, :]

    def block(ref, p):
        return ref[p * 64 : p * 64 + 64, :]

    def first_of(acc):
        return acc + swap(acc)

    def last_of(acc):
        other = swap(acc)
        return jnp.where(half64, acc - other, other - acc)

    def z_layers(spec, k):
        acc = weight(k, 0) * block(spec, 0)
        for p in range(1, 8):
            acc = acc + weight(k, p) * block(spec, p)
        return acc

    def x_planes(spec, at):
        sx = side_x(at)
        return jnp.concatenate(
            [jnp.sum(sx * block(spec, p), axis=0, keepdims=True) for p in range(8)], axis=0
        )

    def narrow(v):
        return jnp.where(half0, v[:PLANE], v[PLANE:])

    def widen(v):
        other = swap(v)
        return jnp.concatenate(
            [jnp.where(half0, v, other), jnp.where(half0, other, v)], axis=0
        )

    def z_ghosts(below, above):
        return below + jnp.where(half64, above, -above)

    def layer_response(both, ghost):
        acc = tab[T_ALPHA : T_ALPHA + 64, :] * both
        for p in range(8):
            acc = acc + resp[rows(g * 512 + p * 64, 64), :] * ghost[p : p + 1, :]
        return acc

    def plane_response(both, ghost):
        side = jnp.concatenate(
            [
                jnp.sum(resp[rows((1 - g) * 512 + p * 64, 64), :] * both, axis=0, keepdims=True)
                for p in range(8)
            ],
            axis=0,
        )
        return side + tab[T_GAMMA : T_GAMMA + 8, :] * ghost

    Z_HIGH, Z_LOW, Z_HIGH2, Z_LOW2, Z_DLOW, Z_DHIGH = range(6)

    def solve(s):
        own = prs.at[s]
        z_forward(ybuf)
        ybuf[...] = y_transform(ybuf[...])
        for p in range(8):
            v = x_forward(
                ybuf[2 * p * PLANE : (2 * p + 1) * PLANE, :],
                ybuf[(2 * p + 1) * PLANE : (2 * p + 2) * PLANE, :],
            )
            hat1[p * 64 : p * 64 + 64, :] = v * modes(p)
        acc = z_layers(hat1, 0)
        first, last = first_of(acc), last_of(acc)
        plane = z_plane(y_transform(x_planes(hat1, T_SX)))
        zsend[s, 0, 0:PLANE, :] = narrow(first)
        zsend[s, 1, 0:PLANE, :] = narrow(last)
        zsend[s, 0, PLANE : PLANE + 8, :] = plane
        zsend[s, 1, PLANE : PLANE + 8, :] = plane

        def layer(side):
            return zsend.at[s, side, pl.ds(0, PLANE)]

        def into(slot):
            return zrecv.at[s, slot, pl.ds(0, PLANE)]

        copies = [
            Message(LOW, layer(0), into(Z_HIGH)),
            Message(HIGH, layer(1), into(Z_LOW)),
            Message(DLOW, zsend.at[s, 0], zrecv.at[s, Z_DHIGH]),
            Message(DHIGH, zsend.at[s, 1], zrecv.at[s, Z_DLOW]),
            Message(LOW2, layer(0), into(Z_HIGH2)),
            Message(HIGH2, layer(1), into(Z_LOW2)),
            Message(PARTNER, zsend.at[s, 0, pl.ds(PLANE, 8)], qrecv.at[s, 3]),
        ]
        for copy in copies:
            copy.start()
        mine = z_plane(gather(plane, 1))
        for copy in copies:
            copy.wait_recv()

        def got(slot):
            return zrecv[s, slot, 0:PLANE, :]

        def got_plane(slot):
            return zrecv[s, slot, PLANE : PLANE + 8, :]

        ghosts = y_transform(
            jnp.concatenate(
                [mine, z_plane(gather(got_plane(Z_DLOW), 2)), z_plane(gather(got_plane(Z_DHIGH), 3))],
                axis=0,
            )
        )
        partner = plane_response(
            z_ghosts(widen(got(Z_DLOW)), widen(got(Z_DHIGH))), ghosts[0:8]
        )
        partner = qrecv[s, 3] + z_plane(y_transform(partner))
        ghost = y_transform(z_plane(gather(partner)))
        above = got(Z_HIGH) + narrow(
            first_of(layer_response(z_ghosts(last, widen(got(Z_HIGH2))), ghosts[16:24]))
        )
        below = got(Z_LOW) + narrow(
            last_of(layer_response(z_ghosts(widen(got(Z_LOW2)), first), ghosts[8:16]))
        )
        above = jnp.where(has_high, above, 0.0)
        below = jnp.where(has_low, below, 0.0)
        both = z_ghosts(widen(below), widen(above))
        sx = side_x()
        for p in range(8):
            extra = weight(0, p) * both + sx * ghost[p : p + 1, :]
            hat[p * 64 : p * 64 + 64, :] = block(hat1, p) + extra * modes(p)
        depth = 3 if s == 0 else 1
        planes = [x_planes(hat, T_SX)]
        if s == 0:
            planes.append(x_planes(hat, T_SX2))
        planes = y_transform(jnp.concatenate(planes, axis=0))
        for i in range(len(planes) // 8):
            qsend[s, i * 8 : i * 8 + 8, :] = z_plane(planes[i * 8 : i * 8 + 8])
        for k in range(depth):
            acc = z_layers(hat, k)
            a, b = x_inverse(jnp.where(half64, first_of(acc), last_of(acc)))
            psend[s, 0, k * PLANE : (k + 1) * PLANE, :] = y_transform(a)
            at = depth - 1 - k
            psend[s, 1, at * PLANE : (at + 1) * PLANE, :] = y_transform(b)
        size = depth * PLANE
        copies = [
            Message(LOW, psend.at[s, 0, pl.ds(0, size)], own.at[pl.ds((CZ + 3) * PLANE, size)]),
            Message(HIGH, psend.at[s, 1, pl.ds(0, size)], own.at[pl.ds((3 - depth) * PLANE, size)]),
        ]
        if s == 0:
            copies += [
                Message(DLOW, qsend.at[s, pl.ds(0, 8)], qrecv.at[s, 2]),
                Message(DHIGH, qsend.at[s, pl.ds(0, 8)], qrecv.at[s, 1]),
                Message(PARTNER, qsend.at[s], psel.at[0]),
            ]
        else:
            copies.append(Message(PARTNER, qsend.at[s, pl.ds(0, 8)], qrecv.at[s, 0]))
        for copy in copies:
            copy.start()
        for p in range(8):
            a, b = x_inverse(block(hat, p))
            ybuf[2 * p * PLANE : (2 * p + 1) * PLANE, :] = a
            ybuf[(2 * p + 1) * PLANE : (2 * p + 2) * PLANE, :] = b
        ybuf[...] = y_transform(ybuf[...])
        z_inverse(ybuf, own, 3 * PLANE)
        for copy in copies:
            copy.wait_recv()
        return copies

    def correct_plane(s, k, into, at_of):
        own = prs.at[s]
        p = own[rows((k + 3) * PLANE, PLANE), :]
        above = own[rows((k + 4) * PLANE, PLANE), :]
        below = own[rows((k + 2) * PLANE, PLANE), :]
        east, west = x_sides(p, xg[pl.ds(16 + k, 1), :])
        north, south = y_sides(p)
        for f, (a, b) in enumerate(((east, west), (north, south), (above, below))):
            at = rows(at_of(k, f), PLANE)
            into[at, :] = into[at, :] - 0.5 * (a - b)

    table_loads[0].wait()
    early = send_fields(fld0, 0)
    maps = [
        Message(PARTNER, idx.at[0], idx.at[1]),
        Message(HIGH, idx.at[0], idx.at[2]),
        Message(LOW, idx.at[0], idx.at[3]),
    ]
    for copy in maps:
        copy.start()
    loads[FIELDS].wait()

    def load_burn(b, lanes):
        return bnn[b * 8 : b * 8 + 8, lanes]

    def store_burn(k, r, v):
        burning[rows(k * PLANE + r, 8), :] = v

    to_layers(load_burn, store_burn)
    for copy in table_loads[1:]:
        copy.wait()
    for side in range(2):
        sx = tab[T_SX + side * 64 : T_SX + side * 64 + 64, :]
        for p in range(8):
            start = side * 512 + p * 64
            resp[start : start + 64, :] = modes(p) * weight(0, p) * sx

    def finish0(k, f, c, change):
        fld1[rows(level(k, f), PLANE), :] = c + change

    early[2].wait_recv()
    for f in range(FIELDS):
        spread(gather(frecv[0, f * 8 : f * 8 + 8, :]), XG + f * 16)

    @pl.loop(2, CZ - 2)
    def _(k):
        tendency_plane(fld0, k, finish0)

    early[0].wait_recv()
    early[1].wait_recv()

    @pl.loop(0, 4)
    def _(i):
        tendency_plane(fld0, i + (CZ - 4) * (i // 2), finish0)

    early = send_fields(fld1, 1)
    for copy in maps:
        copy.wait_recv()
    solve(0)

    near = psel[0, 0:8, :]
    beside = psel[0, 8:16, :]
    spread(gather(near), 16)
    spread(gather(qrecv[0, 1], 2), 0)
    spread(gather(qrecv[0, 2], 3), 32)
    for copy in early:
        copy.wait_recv()
    for copy in early:
        copy.wait_send()
    sides = gather(qsend[0, 0:8, :], 1)
    sign = jnp.where(fine, -0.5, 0.5)
    new0 = frecv[1, 0:8, :] - sign * (sides - beside)
    lane8 = lax.broadcasted_iota(jnp.int32, (8, 128), 1)
    north = jnp.where((lane8 == 63) | (lane8 == 127), 0.0, pltpu.roll(near, 127, 1))
    south = jnp.where((lane8 == 0) | (lane8 == 64), 0.0, pltpu.roll(near, 1, 1))
    new1 = frecv[1, 8:16, :] - 0.5 * (north - south)
    other = swap(near)
    up = pltpu.roll(other, 7, 0)
    down = pltpu.roll(other, 1, 0)
    over = jnp.broadcast_to(swap(qrecv[0, 2])[0:1, :], (8, 128))
    under = jnp.broadcast_to(swap(qrecv[0, 1])[7:8, :], (8, 128))
    above = jnp.where(half8, other, jnp.where(sub8 == 7, over, up))
    below = jnp.where(half8, jnp.where(sub8 == 0, under, down), other)
    new2 = frecv[1, 16:24, :] - 0.5 * (above - below)
    for f, v in enumerate((new0, new1, new2, frecv[1, 24:32, :], frecv[1, 32:40, :])):
        spread(gather(v), XG + f * 16)

    @pl.loop(0, CZ)
    def _(k):
        correct_plane(0, k, fld1, level)

    @pl.when(has_low)
    def _():
        @pl.loop(-2, 0)
        def _(k):
            correct_plane(0, k, fld1, level)

    @pl.when(has_high)
    def _():
        @pl.loop(CZ, CZ + 2)
        def _(k):
            correct_plane(0, k, fld1, level)

    def finish1(k, f, c, change):
        start = fld0[rows(level(k, f), PLANE), :]
        fields[rows((k * FIELDS + f) * PLANE, PLANE), :] = 0.5 * (start + c + change)

    @pl.loop(0, CZ)
    def _(k):
        tendency_plane(fld1, k, finish1)

    solve(1)
    spread(gather(qrecv[1, 0]), 16)

    @pl.loop(0, CZ)
    def _(k):
        correct_plane(1, k, fields, lambda k, f: (k * FIELDS + f) * PLANE)

    for f in range(FIELDS):
        def load_field(k, r, f=f):
            return fields[rows((k * FIELDS + f) * PLANE + r, 8), :]

        def store_field(b, lanes, v, f=f):
            out_s[f, b * 8 : b * 8 + 8, lanes] = v

        to_native(load_field, store_field)

    def store_head(b, lanes, v):
        out_p[b * 8 : b * 8 + 8, lanes] = v

    to_native(lambda k, r: prs[1, rows((k + 3) * PLANE + r, 8), :], store_head)
    for copy in messages:
        copy.wait_send()


def step(state, burn, fmap):
    hbm = pl.BlockSpec(memory_space=pltpu.HBM)
    vmem = pl.BlockSpec(memory_space=pltpu.VMEM)
    tab, bh, bl = tables()
    vm = pltpu.VMEM
    layers = (CZ + 2 * HALO) * LEVEL
    return pl.pallas_call(
        kernel,
        out_shape=(
            jax.ShapeDtypeStruct((FIELDS, CZ, NX * NY), F32),
            jax.ShapeDtypeStruct((CZ, NX * NY), F32),
        ),
        in_specs=[hbm] * 6,
        out_specs=(vmem, vmem),
        scratch_shapes=[
            vm((FIELDS, CZ, NX * NY), F32),
            vm((CZ, NX * NY), F32),
            vm((layers, 128), F32),
            vm((layers, 128), F32),
            vm((CZ * LEVEL, 128), F32),
            vm((CZ * PLANE, 128), F32),
            vm((CZ * PLANE, 128), F32),
            vm((CZ * PLANE, 128), F32),
            vm((CZ * PLANE, 128), F32),
            vm((CZ * PLANE, 128), F32),
            vm((SECTIONS, (CZ + 6) * PLANE, 128), F32),
            vm((1024, 128), F32),
            vm((FIELDS * 16, 128), F32),
            vm((48 + FIELDS * 16, 128), F32),
            vm((SECTIONS, 2, PLANE + 8, 128), F32),
            vm((SECTIONS, 6, PLANE + 8, 128), F32),
            vm((SECTIONS, 2, 3 * PLANE, 128), F32),
            vm((SECTIONS, 16, 128), F32),
            vm((SECTIONS, 4, 8, 128), F32),
            vm((SECTIONS, FIELDS * 8, 128), F32),
            vm((SECTIONS, FIELDS * 8, 128), F32),
            vm((1, 16, 128), F32),
            vm((T_ROWS, 128), F32),
            vm((B_ROWS, 128), BF16),
            vm((B_ROWS, 128), BF16),
            vm((4, 8, 128), jnp.int32),
            pltpu.SemaphoreType.DMA((FIELDS + 1,)),
            pltpu.SemaphoreType.DMA((4,)),
            pltpu.SemaphoreType.DMA((40,)),
            pltpu.SemaphoreType.DMA((40,)),
        ],
        compiler_params=pltpu.CompilerParams(
            collective_id=0, has_side_effects=True, vmem_limit_bytes=40 << 20
        ),
        name="fire_step",
    )(*[pltpu.with_memory_space_constraint(v, pltpu.HBM) for v in (state, burn, fmap, jnp.asarray(tab), jnp.asarray(bh), jnp.asarray(bl))])


def shards(state, burn_rate, face_map):
    fields, head = step(state[0], burn_rate[0], face_map.reshape(8, 128))
    return fields[None], head[None]


def solution(mesh):
    placed = (P("grp", None, "mesh", None), P("grp", "mesh", None), P("grp", "mesh", None))
    return jax.shard_map(
        shards,
        mesh=mesh,
        in_specs=placed,
        out_specs=(P("grp", None, "mesh", None), P("grp", "mesh", None)),
        check_vma=False,
    )
```

time: 72.8 us -> 51 us (0.70)
  the two profiles are of different devices: /device:TPU:8 before, /device:TPU:128 now
where the time goes in v2:
time: 51 us; the launch traced here: 50.9 us
  Pallas kernels  48.5 us (95%)
  local copies, waits for them, and re-layouts  1.76 us (3%)
  between operations  0.64 us (1%)
    pallas_call x1, Pallas kernels, step(): pl.pallas_call(kernel, out_shape=(jax.ShapeDtypeStruct((FIELDS, CZ, NX *...  48.5 us
    unnamed x2, local copies, waits for them, and re-layouts  1.76 us

profile of v2, /device:TPU:128, one launch (start us, length us, event | category | flops | bytes accessed | tf_op | source)
XLA Modules:
  0.0 50.9 jit_solution(16476290491346573650)
XLA Ops:
  0.6 48.5 %fire_step.1 = (f32[5,16,4096]{2,1,0:T(8,128)S(1)}, f32[16,4096]{1,0:T(8,128)S(1)}) custom-call(f32[5,16,4096]{2,1,0:T(8,128)} %bitcast.7, f32[16,4096]{1,0:T(8,128)} %bitcast.8, s32[8,128]{1,0:T(8,128)} %bitcast.9, f32[992,128]{1,0:T(8,128)} %constant.6.clone.tab_h, bf16[256,128]{1,0:T(8,128)(2,1)} %constant.7.clone.bh_h, bf16[256,128]{1,0:T(8,128)(2,1)} %constant.8.clone.bl_h), custom_call_target="tpu_custom_call" | custom-call | tf_op jit(solution)/shard_map/fire_step/pallas_call | solution.py:725
  49.2 1.1 %copy.10 = f32[1,5,16,4096]{3,2,1,0:T(8,128)} copy(f32[1,5,16,4096]{3,2,1,0:T(8,128)S(1)} %bitcast.5) | data formatting | bytes 2621440
  50.2 0.7 %copy.11 = f32[1,16,4096]{2,1,0:T(8,128)} copy(f32[1,16,4096]{2,1,0:T(8,128)S(1)} %bitcast.6) | data formatting | bytes 524288

commit v3 on v2

--- a/solution.py
+++ b/solution.py
@@ -110,7 +110,7 @@
 def kernel(
     state, burn, fmap, tab_h, bh_h, bl_h, out_s, out_p,
     stn, bnn, fld0, fld1, fields, burning, src, ybuf, hat1, hat, prs, resp,
-    edge, xg, zsend, zrecv, psend, qsend, qrecv, fsend, frecv, psel, tab, bh, bl, idx,
+    turns, xg, zsend, zrecv, psend, qsend, qrecv, fsend, frecv, psel, tab, bh, bl, idx,
     in_sem, t_sem, send_sem, recv_sem,
 ):
     g = lax.axis_index("grp")
@@ -191,7 +191,6 @@
                 barrier, inc=1, device_id=where_to[to], device_id_type=MESH
             ),
         )
-    pl.semaphore_wait(barrier, count)
 
     messages = []
 
@@ -218,12 +217,9 @@
                 guarded(exists[self.to], self.copy.wait_send)
 
     lane = lax.broadcasted_iota(jnp.int32, (PLANE, 128), 1)
-    row = lax.broadcasted_iota(jnp.int32, (PLANE, 128), 0)
     half0 = lane < 64
     y_last = (lane == 63) | (lane == 127)
     y_first = (lane == 0) | (lane == 64)
-    x_last = (row == PLANE - 1) & (lane >= 64)
-    x_first = (row == 0) & half0
     half8 = lax.broadcasted_iota(jnp.int32, (8, 128), 1) < 64
     half64 = lax.broadcasted_iota(jnp.int32, (64, 128), 1) < 64
     sub8 = lax.broadcasted_iota(jnp.int32, (8, 128), 0)
@@ -271,31 +267,35 @@
 
         to_layers(load_state, store_state)
 
-    def pack_edges():
-        for f in range(FIELDS):
-            even = edge[pl.ds(f * 16, 8, stride=2), :]
-            odd = edge[pl.ds(f * 16 + 1, 8, stride=2), :]
-            own = jnp.where(
-                fine, jnp.where(half8, swap(even), odd), jnp.where(half8, even, swap(odd))
-            )
-            yield f, own
-
-    def send_fields(fld, s):
-        copies = [
+    def own_plane(fld, f):
+        at = jnp.where(fine, PLANE - 1, 0)
+        tiles = []
+        for odd in range(2):
+            tile = jnp.zeros((8, 128), F32)
+            for r in range(8):
+                one = fld[pl.ds(level(2 * r + odd, f) + at, 1), :]
+                tile = jnp.where(sub8 == r, jnp.broadcast_to(one, (8, 128)), tile)
+            tiles.append(tile)
+        even, odd = tiles
+        return jnp.where(
+            fine, jnp.where(half8, swap(even), odd), jnp.where(half8, even, swap(odd))
+        )
+
+    def field_messages(fld, s):
+        return [
             Message(LOW, fld.at[pl.ds(level(0, 0), 2 * LEVEL)],
                     fld.at[pl.ds(level(CZ, 0), 2 * LEVEL)]),
             Message(HIGH, fld.at[pl.ds(level(CZ - 2, 0), 2 * LEVEL)],
                     fld.at[pl.ds(level(-2, 0), 2 * LEVEL)]),
             Message(PARTNER, fsend.at[s], frecv.at[s]),
         ]
+
+    def send_fields(fld, s):
+        copies = field_messages(fld, s)
         copies[0].start()
         copies[1].start()
-        at = jnp.where(fine, PLANE - 1, 0)
-        for k in range(CZ):
-            for f in range(FIELDS):
-                edge[pl.ds(f * 16 + k, 1), :] = fld[pl.ds(level(k, f) + at, 1), :]
-        for f, own in pack_edges():
-            fsend[s, f * 8 : f * 8 + 8, :] = own
+        for f in range(FIELDS):
+            fsend[s, f * 8 : f * 8 + 8, :] = own_plane(fld, f)
         copies[2].start()
         return copies
 
@@ -311,18 +311,23 @@
 
     def spread(ghost, base):
         other = swap(ghost)
-        xg[pl.ds(base, 8, stride=2), :] = jnp.where(half8, ghost, other)
-        xg[pl.ds(base + 1, 8, stride=2), :] = jnp.where(half8, other, ghost)
-
-    def x_sides(v, ghost):
-        ghost = jnp.broadcast_to(ghost, (PLANE, 128))
+        even = jnp.where(half8, ghost, other)
+        odd = jnp.where(half8, other, ghost)
+        zero = jnp.zeros_like(ghost)
+        for side in range(2):
+            on = fine if side else jnp.logical_not(fine)
+            xg[side, pl.ds(base, 8, stride=2), :] = jnp.where(on, even, zero)
+            xg[side, pl.ds(base + 1, 8, stride=2), :] = jnp.where(on, odd, zero)
+
+    def x_sides(v, at, slot):
+        base = slot * 48
         turned = swap(v)
-        up = pltpu.roll(turned, PLANE - 1, 0)
-        down = pltpu.roll(turned, 1, 0)
-        zero = jnp.zeros_like(ghost)
-        up = jnp.where(x_last, jnp.where(fine, ghost, zero), up)
-        down = jnp.where(x_first, jnp.where(fine, zero, ghost), down)
-        return jnp.where(half0, turned, up), jnp.where(half0, down, turned)
+        turns[base + 8 : base + 40, :] = turned
+        turns[base + 7 : base + 8, :] = xg[0, pl.ds(at, 1), :]
+        turns[base + 40 : base + 41, :] = xg[1, pl.ds(at, 1), :]
+        down = turns[base + 7 : base + 39, :]
+        up = turns[base + 9 : base + 41, :]
+        return turned, jnp.where(half0, down, up)
 
     def y_sides(v):
         north = jnp.where(y_last, 0.0, pltpu.roll(v, 127, 1))
@@ -330,36 +335,40 @@
         return north, south
 
     XG = 48
+    TAIL = XG + FIELDS * 16
 
     def tendency_plane(fld, k, finish):
         c = [fld[rows(level(k, f), PLANE), :] for f in range(FIELDS)]
         reaction = burning[rows(k * PLANE, PLANE), :] * c[3] * c[4]
         source = EXPANSION * reaction
+        half = jnp.where(half0, 0.5, -0.5)
+        cx = c[0] * (half * -COURANT)
+        cy = c[1] * (-0.5 * COURANT)
+        cz = c[2] * (-COURANT * 2.0 / 3.0)
+        cz2 = c[2] * (COURANT / 12.0)
         for f in range(FIELDS):
             above = fld[rows(level(k + 1, f), PLANE), :]
             below = fld[rows(level(k - 1, f), PLANE), :]
             above2 = fld[rows(level(k + 2, f), PLANE), :]
             below2 = fld[rows(level(k - 2, f), PLANE), :]
-            east, west = x_sides(c[f], xg[pl.ds(XG + f * 16 + k, 1), :])
+            inner, outer = x_sides(c[f], XG + f * 16 + k, f)
             north, south = y_sides(c[f])
-            gx = 0.5 * (east - west)
-            gy = 0.5 * (north - south)
+            dx = inner - outer
+            dy = north - south
             dz = above - below
-            gz = (2.0 / 3.0) * dz - (1.0 / 12.0) * (above2 - below2)
-            lap = (east + west) + (north + south) + (above + below) - 6.0 * c[f]
-            adv = c[0] * gx + c[1] * gy + c[2] * gz
-            change = DIFFUSION * lap - COURANT * adv
+            total = (inner + outer) + (north + south) + (above + below)
+            change = (DIFFUSION * total + cx * dx) + (cy * dy + cz * dz) + cz2 * (above2 - below2)
             if f == 0:
-                source = source - gx
+                source = source - half * dx
             elif f == 1:
-                source = source - gy
+                source = source - 0.5 * dy
             elif f == 2:
                 source = source - 0.5 * dz
             elif f == 3:
                 change = change - reaction
             else:
                 change = change - STOICHIOMETRY * reaction
-            finish(k, f, c[f], change)
+            finish(k, f, c[f] * (1.0 - 6.0 * DIFFUSION) + change)
         src[rows(k * PLANE, PLANE), :] = source
 
     def z_forward(into):
@@ -577,8 +586,6 @@
             ybuf[(2 * p + 1) * PLANE : (2 * p + 2) * PLANE, :] = b
         ybuf[...] = y_transform(ybuf[...])
         z_inverse(ybuf, own, 3 * PLANE)
-        for copy in copies:
-            copy.wait_recv()
         return copies
 
     def correct_plane(s, k, into, at_of):
@@ -586,20 +593,26 @@
         p = own[rows((k + 3) * PLANE, PLANE), :]
         above = own[rows((k + 4) * PLANE, PLANE), :]
         below = own[rows((k + 2) * PLANE, PLANE), :]
-        east, west = x_sides(p, xg[pl.ds(16 + k, 1), :])
+        inner, outer = x_sides(p, 16 + k, 0)
         north, south = y_sides(p)
-        for f, (a, b) in enumerate(((east, west), (north, south), (above, below))):
+        half = jnp.where(half0, 0.5, -0.5)
+        for f, v in enumerate(
+            (half * (inner - outer), 0.5 * (north - south), 0.5 * (above - below))
+        ):
             at = rows(at_of(k, f), PLANE)
-            into[at, :] = into[at, :] - 0.5 * (a - b)
-
+            into[at, :] = into[at, :] - v
+
+    for f in range(FIELDS):
+        fsend[0, f * 8 : f * 8 + 8, :] = own_plane(fld0, f)
     table_loads[0].wait()
-    early = send_fields(fld0, 0)
+    pl.semaphore_wait(barrier, count)
+    early = field_messages(fld0, 0)
     maps = [
         Message(PARTNER, idx.at[0], idx.at[1]),
         Message(HIGH, idx.at[0], idx.at[2]),
         Message(LOW, idx.at[0], idx.at[3]),
     ]
-    for copy in maps:
+    for copy in early + maps:
         copy.start()
     loads[FIELDS].wait()
 
@@ -618,8 +631,8 @@
             start = side * 512 + p * 64
             resp[start : start + 64, :] = modes(p) * weight(0, p) * sx
 
-    def finish0(k, f, c, change):
-        fld1[rows(level(k, f), PLANE), :] = c + change
+    def finish0(k, f, v):
+        fld1[rows(level(k, f), PLANE), :] = v
 
     early[2].wait_recv()
     for f in range(FIELDS):
@@ -639,17 +652,13 @@
     early = send_fields(fld1, 1)
     for copy in maps:
         copy.wait_recv()
-    solve(0)
-
+    final = solve(0)
+
+    final[4].wait_recv()
+    early[2].wait_recv()
     near = psel[0, 0:8, :]
     beside = psel[0, 8:16, :]
     spread(gather(near), 16)
-    spread(gather(qrecv[0, 1], 2), 0)
-    spread(gather(qrecv[0, 2], 3), 32)
-    for copy in early:
-        copy.wait_recv()
-    for copy in early:
-        copy.wait_send()
     sides = gather(qsend[0, 0:8, :], 1)
     sign = jnp.where(fine, -0.5, 0.5)
     new0 = frecv[1, 0:8, :] - sign * (sides - beside)
@@ -658,19 +667,45 @@
     south = jnp.where((lane8 == 0) | (lane8 == 64), 0.0, pltpu.roll(near, 1, 1))
     new1 = frecv[1, 8:16, :] - 0.5 * (north - south)
     other = swap(near)
-    up = pltpu.roll(other, 7, 0)
-    down = pltpu.roll(other, 1, 0)
-    over = jnp.broadcast_to(swap(qrecv[0, 2])[0:1, :], (8, 128))
-    under = jnp.broadcast_to(swap(qrecv[0, 1])[7:8, :], (8, 128))
-    above = jnp.where(half8, other, jnp.where(sub8 == 7, over, up))
-    below = jnp.where(half8, jnp.where(sub8 == 0, under, down), other)
+    up = jnp.where(sub8 == 7, 0.0, pltpu.roll(other, 7, 0))
+    down = jnp.where(sub8 == 0, 0.0, pltpu.roll(other, 1, 0))
+    above = jnp.where(half8, other, up)
+    below = jnp.where(half8, down, other)
     new2 = frecv[1, 16:24, :] - 0.5 * (above - below)
     for f, v in enumerate((new0, new1, new2, frecv[1, 24:32, :], frecv[1, 32:40, :])):
         spread(gather(v), XG + f * 16)
-
-    @pl.loop(0, CZ)
+    for copy in early:
+        copy.wait_send()
+
+    @pl.loop(1, CZ - 1)
     def _(k):
         correct_plane(0, k, fld1, level)
+
+    def finish1(k, f, v):
+        start = fld0[rows(level(k, f), PLANE), :]
+        fields[rows((k * FIELDS + f) * PLANE, PLANE), :] = 0.5 * (start + v)
+
+    @pl.loop(3, CZ - 3)
+    def _(k):
+        tendency_plane(fld1, k, finish1)
+
+    for copy in final[:4] + early[:2]:
+        copy.wait_recv()
+    spread(gather(qrecv[0, 1], 2), 0)
+    spread(gather(qrecv[0, 2], 3), 32)
+    over = jnp.broadcast_to(swap(qrecv[0, 2])[0:1, :], (8, 128))
+    under = jnp.broadcast_to(swap(qrecv[0, 1])[7:8, :], (8, 128))
+    rest = jnp.where(
+        half8,
+        jnp.where(sub8 == 0, 0.5 * under, 0.0),
+        jnp.where(sub8 == 7, -0.5 * over, 0.0),
+    )
+    spread(gather(rest), TAIL)
+    spread(gather(new2 + rest), XG + 2 * 16)
+
+    @pl.loop(0, 2)
+    def _(i):
+        correct_plane(0, i * (CZ - 1), fld1, level)
 
     @pl.when(has_low)
     def _():
@@ -684,36 +719,87 @@
         def _(k):
             correct_plane(0, k, fld1, level)
 
-    def finish1(k, f, c, change):
-        start = fld0[rows(level(k, f), PLANE), :]
-        fields[rows((k * FIELDS + f) * PLANE, PLANE), :] = 0.5 * (start + c + change)
-
-    @pl.loop(0, CZ)
+    @pl.loop(3, CZ - 3)
     def _(k):
-        tendency_plane(fld1, k, finish1)
-
-    solve(1)
+        west, east = xg[0, pl.ds(TAIL + k, 1), :], xg[1, pl.ds(TAIL + k, 1), :]
+        at = jnp.where(fine, PLANE - 1, 0)
+        c = fld1[pl.ds(level(k, 0) + at, 1), :]
+        add = 0.5 * (DIFFUSION * (east + west) - (0.5 * COURANT) * c * (east - west))
+        lanes = lax.broadcasted_iota(jnp.int32, (1, 128), 1)
+        here = jnp.where(fine, lanes, 127 - lanes) >= 64
+        row_at = pl.ds((k * FIELDS + 2) * PLANE + at, 1)
+        fields[row_at, :] = fields[row_at, :] + jnp.where(here, add, 0.0)
+
+    @pl.loop(0, 6)
+    def _(i):
+        tendency_plane(fld1, i + (CZ - 6) * (i // 3), finish1)
+
+    final = solve(1)
+    final[2].wait_recv()
     spread(gather(qrecv[1, 0]), 16)
 
-    @pl.loop(0, CZ)
+    def place(k, f):
+        return (k * FIELDS + f) * PLANE
+
+    @pl.loop(1, CZ - 1)
     def _(k):
-        correct_plane(1, k, fields, lambda k, f: (k * FIELDS + f) * PLANE)
-
-    for f in range(FIELDS):
-        def load_field(k, r, f=f):
-            return fields[rows((k * FIELDS + f) * PLANE + r, 8), :]
-
-        def store_field(b, lanes, v, f=f):
-            out_s[f, b * 8 : b * 8 + 8, lanes] = v
-
-        to_native(load_field, store_field)
+        correct_plane(1, k, fields, place)
 
     def store_head(b, lanes, v):
         out_p[b * 8 : b * 8 + 8, lanes] = v
 
     to_native(lambda k, r: prs[1, rows((k + 3) * PLANE + r, 8), :], store_head)
+
+    def put_field(f):
+        def load_field(k, r):
+            return fields[rows(place(k, f) + r, 8), :]
+
+        def store_field(b, lanes, v):
+            out_s[f, b * 8 : b * 8 + 8, lanes] = v
+
+        to_native(load_field, store_field)
+
+    for f in range(3, FIELDS):
+        put_field(f)
+    for copy in final[:2]:
+        copy.wait_recv()
+
+    @pl.loop(0, 2)
+    def _(i):
+        correct_plane(1, i * (CZ - 1), fields, place)
+
+    for f in range(3):
+        put_field(f)
     for copy in messages:
         copy.wait_send()
+
+
+def finish_kernel(fields, head, out_s, out_p, sems):
+    copies = [
+        pltpu.make_async_copy(fields, out_s, sems.at[0]),
+        pltpu.make_async_copy(head, out_p, sems.at[1]),
+    ]
+    for copy in copies:
+        copy.start()
+    for copy in copies:
+        copy.wait()
+
+
+def write_out(fields, head):
+    hbm = pl.BlockSpec(memory_space=pltpu.HBM)
+    vmem = pl.BlockSpec(memory_space=pltpu.VMEM)
+    return pl.pallas_call(
+        finish_kernel,
+        out_shape=(
+            jax.ShapeDtypeStruct(fields.shape, F32),
+            jax.ShapeDtypeStruct(head.shape, F32),
+        ),
+        in_specs=[vmem, vmem],
+        out_specs=(hbm, hbm),
+        scratch_shapes=[pltpu.SemaphoreType.DMA((2,))],
+        compiler_params=pltpu.CompilerParams(vmem_limit_bytes=1 << 20),
+        name="write_out",
+    )(fields, head)
 
 
 def step(state, burn, fmap):
@@ -743,8 +829,8 @@
             vm((CZ * PLANE, 128), F32),
             vm((SECTIONS, (CZ + 6) * PLANE, 128), F32),
             vm((1024, 128), F32),
-            vm((FIELDS * 16, 128), F32),
-            vm((48 + FIELDS * 16, 128), F32),
+            vm((FIELDS * 48, 128), F32),
+            vm((2, 64 + FIELDS * 16, 128), F32),
             vm((SECTIONS, 2, PLANE + 8, 128), F32),
             vm((SECTIONS, 6, PLANE + 8, 128), F32),
             vm((SECTIONS, 2, 3 * PLANE, 128), F32),
@@ -770,7 +856,7 @@
 
 
 def shards(state, burn_rate, face_map):
-    fields, head = step(state[0], burn_rate[0], face_map.reshape(8, 128))
+    fields, head = write_out(*step(state[0], burn_rate[0], face_map.reshape(8, 128)))
     return fields[None], head[None]
 
 

time: 51 us -> 46.5 us (0.912)
  Pallas kernels: 48.5 us -> 45.3 us
  local copies, waits for them, and re-layouts: 1.76 us -> 0 us
    pallas_call x1, Pallas kernels: 48.5 us -> 44.2 us  [step(): pl.pallas_call(kernel, out_shape=(jax.ShapeDtypeStruct((FIELDS, CZ, NX *...]
    unnamed x2 -> x0, local copies, waits for them, and re-layouts: 1.76 us -> none
    pallas_call x0 -> x1, Pallas kernels: none -> 1.15 us  [write_out(): pl.pallas_call(finish_kernel, out_shape=(jax.ShapeDtypeStruct(fields.shap...]
where the time goes in v3:
time: 46.5 us; the launch traced here: 46 us
  Pallas kernels  45.3 us (97%)
  between operations  0.64 us (1%)
    pallas_call x1, Pallas kernels, step(): pl.pallas_call(kernel, out_shape=(jax.ShapeDtypeStruct((FIELDS, CZ, NX *...  44.2 us
    pallas_call x1, Pallas kernels, write_out(): pl.pallas_call(finish_kernel, out_shape=(jax.ShapeDtypeStruct(fields.shap...  1.15 us

profile of v3, /device:TPU:128, one launch (start us, length us, event | category | flops | bytes accessed | tf_op | source)
XLA Modules:
  0.0 46.0 jit_solution(2732586837950940324)
XLA Ops:
  0.6 44.2 %fire_step.1 = (f32[5,16,4096]{2,1,0:T(8,128)S(1)}, f32[16,4096]{1,0:T(8,128)S(1)}) custom-call(f32[5,16,4096]{2,1,0:T(8,128)} %bitcast.5, f32[16,4096]{1,0:T(8,128)} %bitcast.6, s32[8,128]{1,0:T(8,128)} %bitcast.7, f32[992,128]{1,0:T(8,128)} %constant.6.clone.tab_h, bf16[256,128]{1,0:T(8,128)(2,1)} %constant.7.clone.bh_h, bf16[256,128]{1,0:T(8,128)(2,1)} %constant.8.clone.bl_h), custom_call_target="tpu_custom_call" | custom-call | tf_op jit(solution)/shard_map/fire_step/pallas_call | solution.py:811
  44.8 1.2 %write_out.1 = (f32[5,16,4096]{2,1,0:T(8,128)}, f32[16,4096]{1,0:T(8,128)}) custom-call(f32[5,16,4096]{2,1,0:T(8,128)S(1)} %get-tuple-element.6.fields, f32[16,4096]{1,0:T(8,128)S(1)} %get-tuple-element.7.head), custom_call_target="tpu_custom_call" | custom-call | tf_op jit(solution)/shard_map/write_out/pallas_call | solution.py:791

commit v4 on v3

--- a/solution.py
+++ b/solution.py
@@ -45,7 +45,8 @@
 T_ALPHA = 672
 T_SX = 736
 T_SX2 = 864
-T_ROWS = 992
+T_ZF = 992
+T_ROWS = 1056
 B_Y = 0
 B_XF = 128
 B_XI = 192
@@ -66,6 +67,8 @@
             for r in range(8):
                 tab[T_Z1 + p * 8 + r, lanes] = s16[2 * p + h, 2 * r + h]
                 tab[T_Z2 + p * 8 + r, lanes] = s16[2 * p + 1 - h, 2 * r + h]
+            for k in range(8):
+                tab[T_ZF + p * 8 + k, lanes] = s16[2 * p + h, k] * (-1.0) ** h
             for k in range(3):
                 tab[T_W + 8 * k + p, lanes] = s16[2 * p + h, k]
     for at, places in ((T_SX, (63, 0)), (T_SX2, (62, 1))):
@@ -235,26 +238,19 @@
 
     def to_layers(load, store):
         for b in range(2):
-            @pl.loop(0, 4)
-            def _(t):
-                tiles = jnp.stack(
-                    [
-                        load(b, pl.ds(pl.multiple_of((t * 8 + i) * 128, 128), 128))
-                        for i in range(8)
-                    ]
-                )
+            for t in range(4):
+                tiles = jnp.stack([load(b, pl.ds((t * 8 + i) * 128, 128)) for i in range(8)])
                 turned = jnp.swapaxes(tiles, 0, 1)
                 for i in range(8):
                     store(b * 8 + i, t * 8, turned[i])
 
     def to_native(load, store):
         for b in range(2):
-            @pl.loop(0, 4)
-            def _(t):
+            for t in range(4):
                 tiles = jnp.stack([load(b * 8 + i, t * 8) for i in range(8)])
                 turned = jnp.swapaxes(tiles, 0, 1)
                 for i in range(8):
-                    store(b, pl.ds(pl.multiple_of((t * 8 + i) * 128, 128), 128), turned[i])
+                    store(b, pl.ds((t * 8 + i) * 128, 128), turned[i])
 
     for f in range(FIELDS):
         loads[f].wait()
@@ -337,7 +333,7 @@
     XG = 48
     TAIL = XG + FIELDS * 16
 
-    def tendency_plane(fld, k, finish):
+    def tendency_plane(fld, k, finish, u=0):
         c = [fld[rows(level(k, f), PLANE), :] for f in range(FIELDS)]
         reaction = burning[rows(k * PLANE, PLANE), :] * c[3] * c[4]
         source = EXPANSION * reaction
@@ -351,7 +347,7 @@
             below = fld[rows(level(k - 1, f), PLANE), :]
             above2 = fld[rows(level(k + 2, f), PLANE), :]
             below2 = fld[rows(level(k - 2, f), PLANE), :]
-            inner, outer = x_sides(c[f], XG + f * 16 + k, f)
+            inner, outer = x_sides(c[f], XG + f * 16 + k, u * FIELDS + f)
             north, south = y_sides(c[f])
             dx = inner - outer
             dy = north - south
@@ -371,19 +367,6 @@
             finish(k, f, c[f] * (1.0 - 6.0 * DIFFUSION) + change)
         src[rows(k * PLANE, PLANE), :] = source
 
-    def z_forward(into):
-        @pl.loop(0, 4)
-        def _(t):
-            v = [src[rows(k * PLANE + t * 8, 8), :] for k in range(CZ)]
-            even = [v[k] + v[15 - k] for k in range(8)]
-            odd = [v[k] - v[15 - k] for k in range(8)]
-            for c in range(CZ):
-                part = odd if c % 2 else even
-                total = part[0] * F32(S16[c, 0])
-                for k in range(1, 8):
-                    total = total + part[k] * F32(S16[c, k])
-                into[rows(c * PLANE + t * 8, 8), :] = total
-
     def z_inverse(spec, into, base):
         @pl.loop(0, 4)
         def _(t):
@@ -409,6 +392,23 @@
         v = jnp.concatenate([even, odd], axis=0)
         return dot_left(bh[B_XF : B_XF + 64, :64], bl[B_XF : B_XF + 64, :64], v)
 
+    def transform(first, last):
+        pairs = range(first, 8) if last == 0 else range(last)
+        if last == 0:
+            v = y_transform(src[first * PLANE : (CZ - first) * PLANE, :])
+            planes = {k: v[(k - first) * PLANE : (k - first + 1) * PLANE] for k in range(first, CZ - first)}
+        else:
+            v = y_transform(
+                jnp.concatenate(
+                    [src[: last * PLANE, :], src[(CZ - last) * PLANE : CZ * PLANE, :]], axis=0
+                )
+            )
+            planes = {k: v[k * PLANE : (k + 1) * PLANE] for k in range(last)}
+            for i in range(last):
+                planes[CZ - last + i] = v[(last + i) * PLANE : (last + i + 1) * PLANE]
+        for k in pairs:
+            ybuf[k * 64 : k * 64 + 64, :] = x_forward(planes[k], planes[CZ - 1 - k])
+
     def x_inverse(v):
         v = dot_left(bh[B_XI : B_XI + 64, :64], bl[B_XI : B_XI + 64, :64], v)
         even, odd = v[:PLANE], v[PLANE:]
@@ -416,11 +416,13 @@
 
     def z_plane(v):
         other = swap(v)
-        out = jnp.zeros((8, 128), F32)
+        parts = []
         for p in range(8):
-            out = out + tab[T_Z1 + p * 8 : T_Z1 + p * 8 + 8, :] * v[p : p + 1, :]
-            out = out + tab[T_Z2 + p * 8 : T_Z2 + p * 8 + 8, :] * other[p : p + 1, :]
-        return out
+            parts.append(tab[T_Z1 + p * 8 : T_Z1 + p * 8 + 8, :] * v[p : p + 1, :])
+            parts.append(tab[T_Z2 + p * 8 : T_Z2 + p * 8 + 8, :] * other[p : p + 1, :])
+        while len(parts) > 1:
+            parts = [a + b for a, b in zip(parts[::2], parts[1::2])]
+        return parts[0]
 
     def side_x(at=T_SX):
         return tab[rows(at + g * 64, 64), :]
@@ -485,14 +487,19 @@
 
     def solve(s):
         own = prs.at[s]
-        z_forward(ybuf)
-        ybuf[...] = y_transform(ybuf[...])
-        for p in range(8):
-            v = x_forward(
-                ybuf[2 * p * PLANE : (2 * p + 1) * PLANE, :],
-                ybuf[(2 * p + 1) * PLANE : (2 * p + 2) * PLANE, :],
-            )
-            hat1[p * 64 : p * 64 + 64, :] = v * modes(p)
+        for r in range(8):
+            pairs = []
+            for p in range(8):
+                v = ybuf[p * 64 + r * 8 : p * 64 + r * 8 + 8, :]
+                pairs.append(v + jnp.where(half8, swap(v), -swap(v)))
+            for q in range(8):
+                parts = [
+                    tab[T_ZF + q * 8 + p : T_ZF + q * 8 + p + 1, :] * pairs[p] for p in range(8)
+                ]
+                while len(parts) > 1:
+                    parts = [a + b for a, b in zip(parts[::2], parts[1::2])]
+                at = q * 64 + r * 8
+                hat1[at : at + 8, :] = parts[0] * tab[T_IM + at : T_IM + at + 8, :]
         acc = z_layers(hat1, 0)
         first, last = first_of(acc), last_of(acc)
         plane = z_plane(y_transform(x_planes(hat1, T_SX)))
@@ -518,7 +525,7 @@
         ]
         for copy in copies:
             copy.start()
-        mine = z_plane(gather(plane, 1))
+        mine = y_transform(z_plane(gather(plane, 1)))
         for copy in copies:
             copy.wait_recv()
 
@@ -530,20 +537,20 @@
 
         ghosts = y_transform(
             jnp.concatenate(
-                [mine, z_plane(gather(got_plane(Z_DLOW), 2)), z_plane(gather(got_plane(Z_DHIGH), 3))],
+                [z_plane(gather(got_plane(Z_DLOW), 2)), z_plane(gather(got_plane(Z_DHIGH), 3))],
                 axis=0,
             )
         )
         partner = plane_response(
-            z_ghosts(widen(got(Z_DLOW)), widen(got(Z_DHIGH))), ghosts[0:8]
+            z_ghosts(widen(got(Z_DLOW)), widen(got(Z_DHIGH))), mine
         )
         partner = qrecv[s, 3] + z_plane(y_transform(partner))
         ghost = y_transform(z_plane(gather(partner)))
         above = got(Z_HIGH) + narrow(
-            first_of(layer_response(z_ghosts(last, widen(got(Z_HIGH2))), ghosts[16:24]))
+            first_of(layer_response(z_ghosts(last, widen(got(Z_HIGH2))), ghosts[8:16]))
         )
         below = got(Z_LOW) + narrow(
-            last_of(layer_response(z_ghosts(widen(got(Z_LOW2)), first), ghosts[8:16]))
+            last_of(layer_response(z_ghosts(widen(got(Z_LOW2)), first), ghosts[0:8]))
         )
         above = jnp.where(has_high, above, 0.0)
         below = jnp.where(has_low, below, 0.0)
@@ -588,12 +595,12 @@
         z_inverse(ybuf, own, 3 * PLANE)
         return copies
 
-    def correct_plane(s, k, into, at_of):
+    def correct_plane(s, k, into, at_of, u=0):
         own = prs.at[s]
         p = own[rows((k + 3) * PLANE, PLANE), :]
         above = own[rows((k + 4) * PLANE, PLANE), :]
         below = own[rows((k + 2) * PLANE, PLANE), :]
-        inner, outer = x_sides(p, 16 + k, 0)
+        inner, outer = x_sides(p, 16 + k, u)
         north, south = y_sides(p)
         half = jnp.where(half0, 0.5, -0.5)
         for f, v in enumerate(
@@ -638,20 +645,25 @@
     for f in range(FIELDS):
         spread(gather(frecv[0, f * 8 : f * 8 + 8, :]), XG + f * 16)
 
-    @pl.loop(2, CZ - 2)
-    def _(k):
-        tendency_plane(fld0, k, finish0)
+    @pl.loop(0, 6)
+    def _(i):
+        for u in range(2):
+            tendency_plane(fld0, 2 + 2 * i + u, finish0, u)
+
+    transform(2, 0)
 
     early[0].wait_recv()
     early[1].wait_recv()
 
-    @pl.loop(0, 4)
+    @pl.loop(0, 2)
     def _(i):
-        tendency_plane(fld0, i + (CZ - 4) * (i // 2), finish0)
+        for u in range(2):
+            tendency_plane(fld0, i * (CZ - 2) + u, finish0, u)
 
     early = send_fields(fld1, 1)
     for copy in maps:
         copy.wait_recv()
+    transform(0, 2)
     final = solve(0)
 
     final[4].wait_recv()
@@ -677,17 +689,21 @@
     for copy in early:
         copy.wait_send()
 
-    @pl.loop(1, CZ - 1)
-    def _(k):
-        correct_plane(0, k, fld1, level)
+    @pl.loop(0, 2)
+    def _(i):
+        for u in range(7):
+            correct_plane(0, 1 + 7 * i + u, fld1, level, u)
 
     def finish1(k, f, v):
         start = fld0[rows(level(k, f), PLANE), :]
         fields[rows((k * FIELDS + f) * PLANE, PLANE), :] = 0.5 * (start + v)
 
-    @pl.loop(3, CZ - 3)
-    def _(k):
-        tendency_plane(fld1, k, finish1)
+    @pl.loop(0, 5)
+    def _(i):
+        for u in range(2):
+            tendency_plane(fld1, 3 + 2 * i + u, finish1, u)
+
+    transform(3, 0)
 
     for copy in final[:4] + early[:2]:
         copy.wait_recv()
@@ -703,24 +719,20 @@
     spread(gather(rest), TAIL)
     spread(gather(new2 + rest), XG + 2 * 16)
 
-    @pl.loop(0, 2)
-    def _(i):
-        correct_plane(0, i * (CZ - 1), fld1, level)
+    for u in range(2):
+        correct_plane(0, u * (CZ - 1), fld1, level, u)
 
     @pl.when(has_low)
     def _():
-        @pl.loop(-2, 0)
-        def _(k):
-            correct_plane(0, k, fld1, level)
+        for u in range(2):
+            correct_plane(0, u - 2, fld1, level, u)
 
     @pl.when(has_high)
     def _():
-        @pl.loop(CZ, CZ + 2)
-        def _(k):
-            correct_plane(0, k, fld1, level)
-
-    @pl.loop(3, CZ - 3)
-    def _(k):
+        for u in range(2):
+            correct_plane(0, CZ + u, fld1, level, u)
+
+    for k in range(3, CZ - 3):
         west, east = xg[0, pl.ds(TAIL + k, 1), :], xg[1, pl.ds(TAIL + k, 1), :]
         at = jnp.where(fine, PLANE - 1, 0)
         c = fld1[pl.ds(level(k, 0) + at, 1), :]
@@ -730,10 +742,12 @@
         row_at = pl.ds((k * FIELDS + 2) * PLANE + at, 1)
         fields[row_at, :] = fields[row_at, :] + jnp.where(here, add, 0.0)
 
-    @pl.loop(0, 6)
+    @pl.loop(0, 2)
     def _(i):
-        tendency_plane(fld1, i + (CZ - 6) * (i // 3), finish1)
-
+        for u in range(3):
+            tendency_plane(fld1, i * (CZ - 3) + u, finish1, u)
+
+    transform(0, 3)
     final = solve(1)
     final[2].wait_recv()
     spread(gather(qrecv[1, 0]), 16)
@@ -741,9 +755,10 @@
     def place(k, f):
         return (k * FIELDS + f) * PLANE
 
-    @pl.loop(1, CZ - 1)
-    def _(k):
-        correct_plane(1, k, fields, place)
+    @pl.loop(0, 2)
+    def _(i):
+        for u in range(7):
+            correct_plane(1, 1 + 7 * i + u, fields, place, u)
 
     def store_head(b, lanes, v):
         out_p[b * 8 : b * 8 + 8, lanes] = v
@@ -764,9 +779,8 @@
     for copy in final[:2]:
         copy.wait_recv()
 
-    @pl.loop(0, 2)
-    def _(i):
-        correct_plane(1, i * (CZ - 1), fields, place)
+    for u in range(2):
+        correct_plane(1, u * (CZ - 1), fields, place, u)
 
     for f in range(3):
         put_field(f)
@@ -829,7 +843,7 @@
             vm((CZ * PLANE, 128), F32),
             vm((SECTIONS, (CZ + 6) * PLANE, 128), F32),
             vm((1024, 128), F32),
-            vm((FIELDS * 48, 128), F32),
+            vm((3 * FIELDS * 48, 128), F32),
             vm((2, 64 + FIELDS * 16, 128), F32),
             vm((SECTIONS, 2, PLANE + 8, 128), F32),
             vm((SECTIONS, 6, PLANE + 8, 128), F32),

time: 46.5 us -> 44.1 us (0.948)
  Pallas kernels: 45.3 us -> 42.8 us
    pallas_call x1, Pallas kernels: 44.2 us -> 41.6 us  [step(): pl.pallas_call(kernel, out_shape=(jax.ShapeDtypeStruct((FIELDS, CZ, NX *...]
where the time goes in v4:
time: 44.1 us; the launch traced here: 43.4 us
  Pallas kernels  42.8 us (97%)
  between operations  0.64 us (1%)
    pallas_call x1, Pallas kernels, step(): pl.pallas_call(kernel, out_shape=(jax.ShapeDtypeStruct((FIELDS, CZ, NX *...  41.6 us
    pallas_call x1, Pallas kernels, write_out(): pl.pallas_call(finish_kernel, out_shape=(jax.ShapeDtypeStruct(fields.shap...  1.15 us

profile of v4, /device:TPU:128, one launch (start us, length us, event | category | flops | bytes accessed | tf_op | source)
XLA Modules:
  0.0 43.4 jit_solution(15374476593650392185)
XLA Ops:
  0.6 41.6 %fire_step.1 = (f32[5,16,4096]{2,1,0:T(8,128)S(1)}, f32[16,4096]{1,0:T(8,128)S(1)}) custom-call(f32[5,16,4096]{2,1,0:T(8,128)} %bitcast.5, f32[16,4096]{1,0:T(8,128)} %bitcast.6, s32[8,128]{1,0:T(8,128)} %bitcast.7, f32[1056,128]{1,0:T(8,128)} %constant.6.clone.tab_h, bf16[256,128]{1,0:T(8,128)(2,1)} %constant.7.clone.bh_h, bf16[256,128]{1,0:T(8,128)(2,1)} %constant.8.clone.bl_h), custom_call_target="tpu_custom_call" | custom-call | tf_op jit(solution)/shard_map/fire_step/pallas_call | solution.py:825
  42.2 1.2 %write_out.1 = (f32[5,16,4096]{2,1,0:T(8,128)}, f32[16,4096]{1,0:T(8,128)}) custom-call(f32[5,16,4096]{2,1,0:T(8,128)S(1)} %get-tuple-element.6.fields, f32[16,4096]{1,0:T(8,128)S(1)} %get-tuple-element.7.head), custom_call_target="tpu_custom_call" | custom-call | tf_op jit(solution)/shard_map/write_out/pallas_call | solution.py:805

commit v5 on v4

--- a/solution.py
+++ b/solution.py
@@ -113,7 +113,7 @@
 def kernel(
     state, burn, fmap, tab_h, bh_h, bl_h, out_s, out_p,
     stn, bnn, fld0, fld1, fields, burning, src, ybuf, hat1, hat, prs, resp,
-    turns, xg, zsend, zrecv, psend, qsend, qrecv, fsend, frecv, psel, tab, bh, bl, idx,
+    turns, xg, zsend, zrecv, dsend, drecv, psend, qsend, qrecv, fsend, frecv, psel, tab, bh, bl, idx,
     in_sem, t_sem, send_sem, recv_sem,
 ):
     g = lax.axis_index("grp")
@@ -156,35 +156,40 @@
     def clear(ref, start, size):
         ref[start : start + size, :] = jnp.zeros((size, 128), F32)
 
+    def level(k, f):
+        return (f * (CZ + 2 * HALO) + k + HALO) * PLANE
+
     @pl.when(jnp.logical_not(has_low))
     def _():
-        clear(fld0, 0, 2 * LEVEL)
-        clear(fld1, 0, 2 * LEVEL)
+        for f in range(FIELDS):
+            clear(fld0, level(-2, f), 2 * PLANE)
+            clear(fld1, level(-2, f), 2 * PLANE)
         for s in range(SECTIONS):
             clear(prs.at[s], 0, 3 * PLANE)
-            for part in (1, 4):
-                clear(zrecv.at[s, part], 0, PLANE + 8)
+            clear(zrecv.at[s, 1], 0, PLANE)
+            clear(drecv.at[s, 0], 0, 16)
             clear(qrecv.at[s, 1], 0, 8)
 
     @pl.when(jnp.logical_not(has_high))
     def _():
-        clear(fld0, (CZ + 2) * LEVEL, 2 * LEVEL)
-        clear(fld1, (CZ + 2) * LEVEL, 2 * LEVEL)
+        for f in range(FIELDS):
+            clear(fld0, level(CZ, f), 2 * PLANE)
+            clear(fld1, level(CZ, f), 2 * PLANE)
         for s in range(SECTIONS):
             clear(prs.at[s], (CZ + 3) * PLANE, 3 * PLANE)
-            for part in (0, 5):
-                clear(zrecv.at[s, part], 0, PLANE + 8)
+            clear(zrecv.at[s, 0], 0, PLANE)
+            clear(drecv.at[s, 1], 0, 16)
             clear(qrecv.at[s, 2], 0, 8)
 
     @pl.when(m < 2)
     def _():
         for s in range(SECTIONS):
-            clear(zrecv.at[s, 3], 0, PLANE + 8)
+            clear(zrecv.at[s, 3], 0, PLANE)
 
     @pl.when(m > n - 3)
     def _():
         for s in range(SECTIONS):
-            clear(zrecv.at[s, 2], 0, PLANE + 8)
+            clear(zrecv.at[s, 2], 0, PLANE)
 
     barrier = pltpu.get_barrier_semaphore()
     for to in range(7):
@@ -233,9 +238,6 @@
     def rows(start, size):
         return pl.ds(pl.multiple_of(start, 8), size)
 
-    def level(k, f):
-        return ((k + HALO) * FIELDS + f) * PLANE
-
     def to_layers(load, store):
         for b in range(2):
             for t in range(4):
@@ -251,17 +253,6 @@
                 turned = jnp.swapaxes(tiles, 0, 1)
                 for i in range(8):
                     store(b, pl.ds((t * 8 + i) * 128, 128), turned[i])
-
-    for f in range(FIELDS):
-        loads[f].wait()
-
-        def load_state(b, lanes, f=f):
-            return stn[f, b * 8 : b * 8 + 8, lanes]
-
-        def store_state(k, r, v, f=f):
-            fld0[rows(level(k, f) + r, 8), :] = v
-
-        to_layers(load_state, store_state)
 
     def own_plane(fld, f):
         at = jnp.where(fine, PLANE - 1, 0)
@@ -277,23 +268,13 @@
             fine, jnp.where(half8, swap(even), odd), jnp.where(half8, even, swap(odd))
         )
 
-    def field_messages(fld, s):
+    def halo_messages(fld, f):
         return [
-            Message(LOW, fld.at[pl.ds(level(0, 0), 2 * LEVEL)],
-                    fld.at[pl.ds(level(CZ, 0), 2 * LEVEL)]),
-            Message(HIGH, fld.at[pl.ds(level(CZ - 2, 0), 2 * LEVEL)],
-                    fld.at[pl.ds(level(-2, 0), 2 * LEVEL)]),
-            Message(PARTNER, fsend.at[s], frecv.at[s]),
+            Message(LOW, fld.at[pl.ds(level(0, f), 2 * PLANE)],
+                    fld.at[pl.ds(level(CZ, f), 2 * PLANE)]),
+            Message(HIGH, fld.at[pl.ds(level(CZ - 2, f), 2 * PLANE)],
+                    fld.at[pl.ds(level(-2, f), 2 * PLANE)]),
         ]
-
-    def send_fields(fld, s):
-        copies = field_messages(fld, s)
-        copies[0].start()
-        copies[1].start()
-        for f in range(FIELDS):
-            fsend[s, f * 8 : f * 8 + 8, :] = own_plane(fld, f)
-        copies[2].start()
-        return copies
 
     def gather(plane, who=0):
         index = idx[who]
@@ -470,20 +451,15 @@
     def layer_response(both, ghost):
         acc = tab[T_ALPHA : T_ALPHA + 64, :] * both
         for p in range(8):
-            acc = acc + resp[rows(g * 512 + p * 64, 64), :] * ghost[p : p + 1, :]
+            acc = acc + block(resp, p) * ghost[p : p + 1, :]
         return acc
 
-    def plane_response(both, ghost):
-        side = jnp.concatenate(
-            [
-                jnp.sum(resp[rows((1 - g) * 512 + p * 64, 64), :] * both, axis=0, keepdims=True)
-                for p in range(8)
-            ],
-            axis=0,
+    def plane_response(layer):
+        return jnp.concatenate(
+            [jnp.sum(block(resp, p) * layer, axis=0, keepdims=True) for p in range(8)], axis=0
         )
-        return side + tab[T_GAMMA : T_GAMMA + 8, :] * ghost
-
-    Z_HIGH, Z_LOW, Z_HIGH2, Z_LOW2, Z_DLOW, Z_DHIGH = range(6)
+
+    Z_HIGH, Z_LOW, Z_HIGH2, Z_LOW2 = range(4)
 
     def solve(s):
         own = prs.at[s]
@@ -502,50 +478,64 @@
                 hat1[at : at + 8, :] = parts[0] * tab[T_IM + at : T_IM + at + 8, :]
         acc = z_layers(hat1, 0)
         first, last = first_of(acc), last_of(acc)
-        plane = z_plane(y_transform(x_planes(hat1, T_SX)))
-        zsend[s, 0, 0:PLANE, :] = narrow(first)
-        zsend[s, 1, 0:PLANE, :] = narrow(last)
-        zsend[s, 0, PLANE : PLANE + 8, :] = plane
-        zsend[s, 1, PLANE : PLANE + 8, :] = plane
-
-        def layer(side):
-            return zsend.at[s, side, pl.ds(0, PLANE)]
-
-        def into(slot):
-            return zrecv.at[s, slot, pl.ds(0, PLANE)]
-
+        zsend[s, 0] = narrow(first)
+        zsend[s, 1] = narrow(last)
         copies = [
-            Message(LOW, layer(0), into(Z_HIGH)),
-            Message(HIGH, layer(1), into(Z_LOW)),
-            Message(DLOW, zsend.at[s, 0], zrecv.at[s, Z_DHIGH]),
-            Message(DHIGH, zsend.at[s, 1], zrecv.at[s, Z_DLOW]),
-            Message(LOW2, layer(0), into(Z_HIGH2)),
-            Message(HIGH2, layer(1), into(Z_LOW2)),
-            Message(PARTNER, zsend.at[s, 0, pl.ds(PLANE, 8)], qrecv.at[s, 3]),
+            Message(LOW2, zsend.at[s, 0], zrecv.at[s, Z_HIGH2]),
+            Message(HIGH2, zsend.at[s, 1], zrecv.at[s, Z_LOW2]),
+            Message(LOW, zsend.at[s, 0], zrecv.at[s, Z_HIGH]),
+            Message(HIGH, zsend.at[s, 1], zrecv.at[s, Z_LOW]),
         ]
         for copy in copies:
             copy.start()
+        plane = z_plane(y_transform(x_planes(hat1, T_SX)))
+        dsend[s, 0, 0:8, :] = plane
+        dsend[s, 1, 0:8, :] = plane
+        dsend[s, 0, 8:16, :] = plane_response(first)
+        dsend[s, 1, 8:16, :] = plane_response(last)
+        sides = [
+            Message(DLOW, dsend.at[s, 0], drecv.at[s, 1]),
+            Message(DHIGH, dsend.at[s, 1], drecv.at[s, 0]),
+            Message(PARTNER, dsend.at[s, 0, pl.ds(0, 8)], qrecv.at[s, 3]),
+        ]
+        for copy in sides:
+            copy.start()
+        if s == 0:
+            for f in range(FIELDS):
+                fsend[1, f * 8 : f * 8 + 8, :] = own_plane(fld1, f)
+            early.append(Message(PARTNER, fsend.at[1], frecv.at[1]))
+            for f in range(FIELDS):
+                early.extend(halo_messages(fld1, f))
+            for copy in early:
+                copy.start()
+            for copy in maps[1:]:
+                copy.wait_recv()
         mine = y_transform(z_plane(gather(plane, 1)))
-        for copy in copies:
+        mine = tab[T_GAMMA : T_GAMMA + 8, :] * mine
+        for copy in sides:
             copy.wait_recv()
-
-        def got(slot):
-            return zrecv[s, slot, 0:PLANE, :]
-
-        def got_plane(slot):
-            return zrecv[s, slot, PLANE : PLANE + 8, :]
-
+        response = drecv[s, 0, 8:16, :] + jnp.where(
+            half8, drecv[s, 1, 8:16, :], -drecv[s, 1, 8:16, :]
+        )
+        partner = qrecv[s, 3] + z_plane(y_transform(response + mine))
+        ghost = z_plane(gather(partner))
         ghosts = y_transform(
             jnp.concatenate(
-                [z_plane(gather(got_plane(Z_DLOW), 2)), z_plane(gather(got_plane(Z_DHIGH), 3))],
+                [
+                    z_plane(gather(drecv[s, 0, 0:8, :], 2)),
+                    z_plane(gather(drecv[s, 1, 0:8, :], 3)),
+                    ghost,
+                ],
                 axis=0,
             )
         )
-        partner = plane_response(
-            z_ghosts(widen(got(Z_DLOW)), widen(got(Z_DHIGH))), mine
-        )
-        partner = qrecv[s, 3] + z_plane(y_transform(partner))
-        ghost = y_transform(z_plane(gather(partner)))
+        ghost = ghosts[16:24]
+        for copy in copies:
+            copy.wait_recv()
+
+        def got(slot):
+            return zrecv[s, slot]
+
         above = got(Z_HIGH) + narrow(
             first_of(layer_response(z_ghosts(last, widen(got(Z_HIGH2))), ghosts[8:16]))
         )
@@ -609,17 +599,33 @@
             at = rows(at_of(k, f), PLANE)
             into[at, :] = into[at, :] - v
 
+    early = []
+    for f in range(FIELDS):
+        loads[f].wait()
+
+        def load_state(b, lanes, f=f):
+            return stn[f, b * 8 : b * 8 + 8, lanes]
+
+        def store_state(k, r, v, f=f):
+            fld0[rows(level(k, f) + r, 8), :] = v
+
+        to_layers(load_state, store_state)
+        if f == 0:
+            pl.semaphore_wait(barrier, count)
+        copies = halo_messages(fld0, f)
+        for copy in copies:
+            copy.start()
+        early.extend(copies)
     for f in range(FIELDS):
         fsend[0, f * 8 : f * 8 + 8, :] = own_plane(fld0, f)
     table_loads[0].wait()
-    pl.semaphore_wait(barrier, count)
-    early = field_messages(fld0, 0)
     maps = [
+        Message(PARTNER, fsend.at[0], frecv.at[0]),
         Message(PARTNER, idx.at[0], idx.at[1]),
         Message(HIGH, idx.at[0], idx.at[2]),
         Message(LOW, idx.at[0], idx.at[3]),
     ]
-    for copy in early + maps:
+    for copy in maps:
         copy.start()
     loads[FIELDS].wait()
 
@@ -632,16 +638,13 @@
     to_layers(load_burn, store_burn)
     for copy in table_loads[1:]:
         copy.wait()
-    for side in range(2):
-        sx = tab[T_SX + side * 64 : T_SX + side * 64 + 64, :]
-        for p in range(8):
-            start = side * 512 + p * 64
-            resp[start : start + 64, :] = modes(p) * weight(0, p) * sx
+    for p in range(8):
+        resp[p * 64 : p * 64 + 64, :] = modes(p) * weight(0, p) * side_x()
 
     def finish0(k, f, v):
         fld1[rows(level(k, f), PLANE), :] = v
 
-    early[2].wait_recv()
+    maps[0].wait_recv()
     for f in range(FIELDS):
         spread(gather(frecv[0, f * 8 : f * 8 + 8, :]), XG + f * 16)
 
@@ -652,22 +655,20 @@
 
     transform(2, 0)
 
-    early[0].wait_recv()
-    early[1].wait_recv()
+    for copy in early:
+        copy.wait_recv()
 
     @pl.loop(0, 2)
     def _(i):
         for u in range(2):
             tendency_plane(fld0, i * (CZ - 2) + u, finish0, u)
 
-    early = send_fields(fld1, 1)
-    for copy in maps:
-        copy.wait_recv()
+    early = []
     transform(0, 2)
     final = solve(0)
 
     final[4].wait_recv()
-    early[2].wait_recv()
+    early[0].wait_recv()
     near = psel[0, 0:8, :]
     beside = psel[0, 8:16, :]
     spread(gather(near), 16)
@@ -705,7 +706,7 @@
 
     transform(3, 0)
 
-    for copy in final[:4] + early[:2]:
+    for copy in final[:4] + early[1:]:
         copy.wait_recv()
     spread(gather(qrecv[0, 1], 2), 0)
     spread(gather(qrecv[0, 2], 3), 32)
@@ -842,11 +843,13 @@
             vm((CZ * PLANE, 128), F32),
             vm((CZ * PLANE, 128), F32),
             vm((SECTIONS, (CZ + 6) * PLANE, 128), F32),
-            vm((1024, 128), F32),
+            vm((512, 128), F32),
             vm((3 * FIELDS * 48, 128), F32),
             vm((2, 64 + FIELDS * 16, 128), F32),
-            vm((SECTIONS, 2, PLANE + 8, 128), F32),
-            vm((SECTIONS, 6, PLANE + 8, 128), F32),
+            vm((SECTIONS, 2, PLANE, 128), F32),
+            vm((SECTIONS, 4, PLANE, 128), F32),
+            vm((SECTIONS, 2, 16, 128), F32),
+            vm((SECTIONS, 2, 16, 128), F32),
             vm((SECTIONS, 2, 3 * PLANE, 128), F32),
             vm((SECTIONS, 16, 128), F32),
             vm((SECTIONS, 4, 8, 128), F32),
@@ -859,8 +862,8 @@
             vm((4, 8, 128), jnp.int32),
             pltpu.SemaphoreType.DMA((FIELDS + 1,)),
             pltpu.SemaphoreType.DMA((4,)),
-            pltpu.SemaphoreType.DMA((40,)),
-            pltpu.SemaphoreType.DMA((40,)),
+            pltpu.SemaphoreType.DMA((48,)),
+            pltpu.SemaphoreType.DMA((48,)),
         ],
         compiler_params=pltpu.CompilerParams(
             collective_id=0, has_side_effects=True, vmem_limit_bytes=40 << 20

time: 44.1 us -> 42.2 us (0.957); the launches traced: 43.4 us -> 42.1 us
  Pallas kernels: 42.8 us -> 41.5 us
    pallas_call x1, Pallas kernels: 41.6 us -> 40.3 us  [step(): pl.pallas_call(kernel, out_shape=(jax.ShapeDtypeStruct((FIELDS, CZ, NX *...]
where the time goes in v5:
time: 42.2 us; the launch traced here: 42.1 us
  Pallas kernels  41.5 us (98%)
  between operations  0.64 us (2%)
    pallas_call x1, Pallas kernels, step(): pl.pallas_call(kernel, out_shape=(jax.ShapeDtypeStruct((FIELDS, CZ, NX *...  40.3 us
    pallas_call x1, Pallas kernels, write_out(): pl.pallas_call(finish_kernel, out_shape=(jax.ShapeDtypeStruct(fields.shap...  1.15 us

profile of v5, /device:TPU:128, one launch (start us, length us, event | category | flops | bytes accessed | tf_op | source)
XLA Modules:
  0.0 42.1 jit_solution(4003892042191213410)
XLA Ops:
  0.6 40.3 %fire_step.1 = (f32[5,16,4096]{2,1,0:T(8,128)S(1)}, f32[16,4096]{1,0:T(8,128)S(1)}) custom-call(f32[5,16,4096]{2,1,0:T(8,128)} %bitcast.5, f32[16,4096]{1,0:T(8,128)} %bitcast.6, s32[8,128]{1,0:T(8,128)} %bitcast.7, f32[1056,128]{1,0:T(8,128)} %constant.6.clone.tab_h, bf16[256,128]{1,0:T(8,128)(2,1)} %constant.7.clone.bh_h, bf16[256,128]{1,0:T(8,128)(2,1)} %constant.8.clone.bl_h), custom_call_target="tpu_custom_call" | custom-call | tf_op jit(solution)/shard_map/fire_step/pallas_call | solution.py:826
  41.0 1.2 %write_out.1 = (f32[5,16,4096]{2,1,0:T(8,128)}, f32[16,4096]{1,0:T(8,128)}) custom-call(f32[5,16,4096]{2,1,0:T(8,128)S(1)} %get-tuple-element.6.fields, f32[16,4096]{1,0:T(8,128)S(1)} %get-tuple-element.7.head), custom_call_target="tpu_custom_call" | custom-call | tf_op jit(solution)/shard_map/write_out/pallas_call | solution.py:806

commit v6 on v5

--- a/solution.py
+++ b/solution.py
@@ -488,7 +488,8 @@
         ]
         for copy in copies:
             copy.start()
-        plane = z_plane(y_transform(x_planes(hat1, T_SX)))
+        start = x_planes(hat1, T_SX)
+        plane = z_plane(y_transform(start))
         dsend[s, 0, 0:8, :] = plane
         dsend[s, 1, 0:8, :] = plane
         dsend[s, 0, 8:16, :] = plane_response(first)
@@ -545,38 +546,54 @@
         above = jnp.where(has_high, above, 0.0)
         below = jnp.where(has_low, below, 0.0)
         both = z_ghosts(widen(below), widen(above))
-        sx = side_x()
-        for p in range(8):
-            extra = weight(0, p) * both + sx * ghost[p : p + 1, :]
-            hat[p * 64 : p * 64 + 64, :] = block(hat1, p) + extra * modes(p)
         depth = 3 if s == 0 else 1
-        planes = [x_planes(hat, T_SX)]
-        if s == 0:
-            planes.append(x_planes(hat, T_SX2))
-        planes = y_transform(jnp.concatenate(planes, axis=0))
-        for i in range(len(planes) // 8):
-            qsend[s, i * 8 : i * 8 + 8, :] = z_plane(planes[i * 8 : i * 8 + 8])
-        for k in range(depth):
-            acc = z_layers(hat, k)
+        size = depth * PLANE
+
+        def spectrum():
+            sx = side_x()
+            for p in range(8):
+                extra = weight(0, p) * both + sx * ghost[p : p + 1, :]
+                hat[p * 64 : p * 64 + 64, :] = block(hat1, p) + extra * modes(p)
+
+        def layers_out(k, acc):
             a, b = x_inverse(jnp.where(half64, first_of(acc), last_of(acc)))
             psend[s, 0, k * PLANE : (k + 1) * PLANE, :] = y_transform(a)
             at = depth - 1 - k
             psend[s, 1, at * PLANE : (at + 1) * PLANE, :] = y_transform(b)
-        size = depth * PLANE
-        copies = [
+
+        stack = [
             Message(LOW, psend.at[s, 0, pl.ds(0, size)], own.at[pl.ds((CZ + 3) * PLANE, size)]),
             Message(HIGH, psend.at[s, 1, pl.ds(0, size)], own.at[pl.ds((3 - depth) * PLANE, size)]),
         ]
         if s == 0:
-            copies += [
+            spectrum()
+            planes = y_transform(
+                jnp.concatenate([x_planes(hat, T_SX), x_planes(hat, T_SX2)], axis=0)
+            )
+            for i in range(2):
+                qsend[s, i * 8 : i * 8 + 8, :] = z_plane(planes[i * 8 : i * 8 + 8])
+            copies = [
                 Message(DLOW, qsend.at[s, pl.ds(0, 8)], qrecv.at[s, 2]),
                 Message(DHIGH, qsend.at[s, pl.ds(0, 8)], qrecv.at[s, 1]),
                 Message(PARTNER, qsend.at[s], psel.at[0]),
             ]
+            for copy in copies:
+                copy.start()
+            for k in range(depth):
+                layers_out(k, z_layers(hat, k))
+            for copy in stack:
+                copy.start()
         else:
-            copies.append(Message(PARTNER, qsend.at[s, pl.ds(0, 8)], qrecv.at[s, 0]))
-        for copy in copies:
-            copy.start()
+            layers_out(0, acc + layer_response(both, ghost))
+            for copy in stack:
+                copy.start()
+            plane = start + plane_response(both) + tab[T_GAMMA : T_GAMMA + 8, :] * ghost
+            qsend[s, 0:8, :] = z_plane(y_transform(plane))
+            copies = [Message(PARTNER, qsend.at[s, pl.ds(0, 8)], qrecv.at[s, 0])]
+            for copy in copies:
+                copy.start()
+            spectrum()
+        copies = stack + copies
         for p in range(8):
             a, b = x_inverse(block(hat, p))
             ybuf[2 * p * PLANE : (2 * p + 1) * PLANE, :] = a
@@ -585,19 +602,23 @@
         z_inverse(ybuf, own, 3 * PLANE)
         return copies
 
-    def correct_plane(s, k, into, at_of, u=0):
+    def correct_z(s, k, into, at_of):
         own = prs.at[s]
-        p = own[rows((k + 3) * PLANE, PLANE), :]
         above = own[rows((k + 4) * PLANE, PLANE), :]
         below = own[rows((k + 2) * PLANE, PLANE), :]
+        at = rows(at_of(k, 2), PLANE)
+        into[at, :] = into[at, :] - 0.5 * (above - below)
+
+    def correct_plane(s, k, into, at_of, u=0, along_z=True):
+        p = prs[s, rows((k + 3) * PLANE, PLANE), :]
         inner, outer = x_sides(p, 16 + k, u)
         north, south = y_sides(p)
         half = jnp.where(half0, 0.5, -0.5)
-        for f, v in enumerate(
-            (half * (inner - outer), 0.5 * (north - south), 0.5 * (above - below))
-        ):
+        for f, v in enumerate((half * (inner - outer), 0.5 * (north - south))):
             at = rows(at_of(k, f), PLANE)
             into[at, :] = into[at, :] - v
+        if along_z:
+            correct_z(s, k, into, at_of)
 
     early = []
     for f in range(FIELDS):
@@ -761,6 +782,9 @@
         for u in range(7):
             correct_plane(1, 1 + 7 * i + u, fields, place, u)
 
+    for u in range(2):
+        correct_plane(1, u * (CZ - 1), fields, place, u, along_z=False)
+
     def store_head(b, lanes, v):
         out_p[b * 8 : b * 8 + 8, lanes] = v
 
@@ -775,16 +799,13 @@
 
         to_native(load_field, store_field)
 
-    for f in range(3, FIELDS):
+    for f in (0, 1, 3, 4):
         put_field(f)
     for copy in final[:2]:
         copy.wait_recv()
-
     for u in range(2):
-        correct_plane(1, u * (CZ - 1), fields, place, u)
-
-    for f in range(3):
-        put_field(f)
+        correct_z(1, u * (CZ - 1), fields, place)
+    put_field(2)
     for copy in messages:
         copy.wait_send()
 

time: 42.2 us -> 42.2 us (level)
  no operation moved by 1% of the time
where the time goes in v6:
time: 42.2 us; the launch traced here: 42.1 us
  Pallas kernels  41.5 us (98%)
  between operations  0.64 us (2%)
    pallas_call x1, Pallas kernels, step(): pl.pallas_call(kernel, out_shape=(jax.ShapeDtypeStruct((FIELDS, CZ, NX *...  40.3 us
    pallas_call x1, Pallas kernels, write_out(): pl.pallas_call(finish_kernel, out_shape=(jax.ShapeDtypeStruct(fields.shap...  1.15 us

profile of v6, /device:TPU:128, one launch (start us, length us, event | category | flops | bytes accessed | tf_op | source)
XLA Modules:
  0.0 42.1 jit_solution(8183684977313428387)
XLA Ops:
  0.6 40.3 %fire_step.1 = (f32[5,16,4096]{2,1,0:T(8,128)S(1)}, f32[16,4096]{1,0:T(8,128)S(1)}) custom-call(f32[5,16,4096]{2,1,0:T(8,128)} %bitcast.5, f32[16,4096]{1,0:T(8,128)} %bitcast.6, s32[8,128]{1,0:T(8,128)} %bitcast.7, f32[1056,128]{1,0:T(8,128)} %constant.6.clone.tab_h, bf16[256,128]{1,0:T(8,128)(2,1)} %constant.7.clone.bh_h, bf16[256,128]{1,0:T(8,128)(2,1)} %constant.8.clone.bl_h), custom_call_target="tpu_custom_call" | custom-call | tf_op jit(solution)/shard_map/fire_step/pallas_call | solution.py:847
  40.9 1.2 %write_out.1 = (f32[5,16,4096]{2,1,0:T(8,128)}, f32[16,4096]{1,0:T(8,128)}) custom-call(f32[5,16,4096]{2,1,0:T(8,128)S(1)} %get-tuple-element.6.fields, f32[16,4096]{1,0:T(8,128)S(1)} %get-tuple-element.7.head), custom_call_target="tpu_custom_call" | custom-call | tf_op jit(solution)/shard_map/write_out/pallas_call | solution.py:827

commit v7 on v6

--- a/solution.py
+++ b/solution.py
@@ -389,6 +389,27 @@
                 planes[CZ - last + i] = v[(last + i) * PLANE : (last + i + 1) * PLANE]
         for k in pairs:
             ybuf[k * 64 : k * 64 + 64, :] = x_forward(planes[k], planes[CZ - 1 - k])
+        for r in range(8):
+            turned = []
+            for p in pairs:
+                v = ybuf[p * 64 + r * 8 : p * 64 + r * 8 + 8, :]
+                turned.append(v + jnp.where(half8, swap(v), -swap(v)))
+            for q in range(8):
+                at = q * 64 + r * 8
+                parts = [
+                    tab[T_ZF + q * 8 + p : T_ZF + q * 8 + p + 1, :] * v
+                    for p, v in zip(pairs, turned)
+                ]
+                if last:
+                    parts.append(hat1[at : at + 8, :])
+                while len(parts) > 1:
+                    parts = [a + b for a, b in zip(parts[::2], parts[1::2])] + (
+                        parts[-1:] if len(parts) % 2 else []
+                    )
+                total = parts[0]
+                if last:
+                    total = total * tab[T_IM + at : T_IM + at + 8, :]
+                hat1[at : at + 8, :] = total
 
     def x_inverse(v):
         v = dot_left(bh[B_XI : B_XI + 64, :64], bl[B_XI : B_XI + 64, :64], v)
@@ -463,19 +484,6 @@
 
     def solve(s):
         own = prs.at[s]
-        for r in range(8):
-            pairs = []
-            for p in range(8):
-                v = ybuf[p * 64 + r * 8 : p * 64 + r * 8 + 8, :]
-                pairs.append(v + jnp.where(half8, swap(v), -swap(v)))
-            for q in range(8):
-                parts = [
-                    tab[T_ZF + q * 8 + p : T_ZF + q * 8 + p + 1, :] * pairs[p] for p in range(8)
-                ]
-                while len(parts) > 1:
-                    parts = [a + b for a, b in zip(parts[::2], parts[1::2])]
-                at = q * 64 + r * 8
-                hat1[at : at + 8, :] = parts[0] * tab[T_IM + at : T_IM + at + 8, :]
         acc = z_layers(hat1, 0)
         first, last = first_of(acc), last_of(acc)
         zsend[s, 0] = narrow(first)
@@ -679,10 +687,8 @@
     for copy in early:
         copy.wait_recv()
 
-    @pl.loop(0, 2)
-    def _(i):
-        for u in range(2):
-            tendency_plane(fld0, i * (CZ - 2) + u, finish0, u)
+    for u, k in enumerate((0, 1, CZ - 2, CZ - 1)):
+        tendency_plane(fld0, k, finish0, u)
 
     early = []
     transform(0, 2)
@@ -865,7 +871,7 @@
             vm((CZ * PLANE, 128), F32),
             vm((SECTIONS, (CZ + 6) * PLANE, 128), F32),
             vm((512, 128), F32),
-            vm((3 * FIELDS * 48, 128), F32),
+            vm((7 * FIELDS * 48, 128), F32),
             vm((2, 64 + FIELDS * 16, 128), F32),
             vm((SECTIONS, 2, PLANE, 128), F32),
             vm((SECTIONS, 4, PLANE, 128), F32),

time: 42.2 us -> 42 us (level)
  no operation moved by 1% of the time
where the time goes in v7:
time: 42 us; the launch traced here: 41.9 us
  Pallas kernels  41.2 us (98%)
  between operations  0.64 us (2%)
    pallas_call x1, Pallas kernels, step(): pl.pallas_call(kernel, out_shape=(jax.ShapeDtypeStruct((FIELDS, CZ, NX *...  40.1 us
    pallas_call x1, Pallas kernels, write_out(): pl.pallas_call(finish_kernel, out_shape=(jax.ShapeDtypeStruct(fields.shap...  1.15 us

profile of v7, /device:TPU:128, one launch (start us, length us, event | category | flops | bytes accessed | tf_op | source)
XLA Modules:
  0.0 41.9 jit_solution(16208660621145176610)
XLA Ops:
  0.6 40.1 %fire_step.1 = (f32[5,16,4096]{2,1,0:T(8,128)S(1)}, f32[16,4096]{1,0:T(8,128)S(1)}) custom-call(f32[5,16,4096]{2,1,0:T(8,128)} %bitcast.5, f32[16,4096]{1,0:T(8,128)} %bitcast.6, s32[8,128]{1,0:T(8,128)} %bitcast.7, f32[1056,128]{1,0:T(8,128)} %constant.6.clone.tab_h, bf16[256,128]{1,0:T(8,128)(2,1)} %constant.7.clone.bh_h, bf16[256,128]{1,0:T(8,128)(2,1)} %constant.8.clone.bl_h), custom_call_target="tpu_custom_call" | custom-call | tf_op jit(solution)/shard_map/fire_step/pallas_call | solution.py:853
  40.7 1.2 %write_out.1 = (f32[5,16,4096]{2,1,0:T(8,128)}, f32[16,4096]{1,0:T(8,128)}) custom-call(f32[5,16,4096]{2,1,0:T(8,128)S(1)} %get-tuple-element.6.fields, f32[16,4096]{1,0:T(8,128)S(1)} %get-tuple-element.7.head), custom_call_target="tpu_custom_call" | custom-call | tf_op jit(solution)/shard_map/write_out/pallas_call | solution.py:833

commit v8 on v7

--- a/solution.py
+++ b/solution.py
@@ -872,7 +872,7 @@
             vm((SECTIONS, (CZ + 6) * PLANE, 128), F32),
             vm((512, 128), F32),
             vm((7 * FIELDS * 48, 128), F32),
-            vm((2, 64 + FIELDS * 16, 128), F32),
+            vm((2, 80 + FIELDS * 16, 128), F32),
             vm((SECTIONS, 2, PLANE, 128), F32),
             vm((SECTIONS, 4, PLANE, 128), F32),
             vm((SECTIONS, 2, 16, 128), F32),

time: 42 us -> 42 us (level)
  no operation moved by 1% of the time
where the time goes in v8:
time: 42 us; the launch traced here: 41.9 us
  Pallas kernels  41.2 us (98%)
  between operations  0.64 us (2%)
    pallas_call x1, Pallas kernels, step(): pl.pallas_call(kernel, out_shape=(jax.ShapeDtypeStruct((FIELDS, CZ, NX *...  40.1 us
    pallas_call x1, Pallas kernels, write_out(): pl.pallas_call(finish_kernel, out_shape=(jax.ShapeDtypeStruct(fields.shap...  1.15 us

profile of v8, /device:TPU:128, one launch (start us, length us, event | category | flops | bytes accessed | tf_op | source)
XLA Modules:
  0.0 41.9 jit_solution(14329456078737688112)
XLA Ops:
  0.6 40.1 %fire_step.1 = (f32[5,16,4096]{2,1,0:T(8,128)S(1)}, f32[16,4096]{1,0:T(8,128)S(1)}) custom-call(f32[5,16,4096]{2,1,0:T(8,128)} %bitcast.5, f32[16,4096]{1,0:T(8,128)} %bitcast.6, s32[8,128]{1,0:T(8,128)} %bitcast.7, f32[1056,128]{1,0:T(8,128)} %constant.6.clone.tab_h, bf16[256,128]{1,0:T(8,128)(2,1)} %constant.7.clone.bh_h, bf16[256,128]{1,0:T(8,128)(2,1)} %constant.8.clone.bl_h), custom_call_target="tpu_custom_call" | custom-call | tf_op jit(solution)/shard_map/fire_step/pallas_call | solution.py:853
  40.7 1.2 %write_out.1 = (f32[5,16,4096]{2,1,0:T(8,128)}, f32[16,4096]{1,0:T(8,128)}) custom-call(f32[5,16,4096]{2,1,0:T(8,128)S(1)} %get-tuple-element.6.fields, f32[16,4096]{1,0:T(8,128)S(1)} %get-tuple-element.7.head), custom_call_target="tpu_custom_call" | custom-call | tf_op jit(solution)/shard_map/write_out/pallas_call | solution.py:833
